TPU v7x, 128 devices: a whole 4x4x4 slice. The times are simulated.
128 devices in a mesh: blk: 64 (over x, y, z_lo, core), grp: 2 (over z_hi).
Axes of the slice: x: 4, y: 4, z: 4 (z_hi: 2, z_lo: 2; z = z_hi * 2 + z_lo), core: 2. Of those that a mesh axis runs over, the one named last changes fastest.
Arguments:
- sky_maps: float32 [4, 512, 4096], P(None, ('blk', 'grp')), may hold values from -6 to 6
- legendre: bfloat16 [512, 512, 2048], P(('blk', 'grp')), may hold values from -0.25 to 0.25
- owner_table: int32 [512], replicated, may hold values from 0 to 511, each once
Outputs:
- harmonics: float32 [512, 4, 2, 2048], P(('blk', 'grp'))
- spectra: float32 [10, 2048], P(None, ('blk', 'grp'))
Inputs may be any that keep to these rules, and one draw needn't show every extreme that they name: `owner_table`: a permutation of the orders 0 to 511.
All inputs are finite; a program needn't handle non-finite values.
Results may differ from a plain program's by a relative error of at most 0.0034.
Values may be sent and summed in bfloat16 or wider, within the bound.
A program may use at most 128 MiB of HBM per device.

v0:
```python
import functools
import math

import jax
import jax.numpy as jnp
import numpy as np
from jax import lax
from jax.experimental import pallas as pl
from jax.experimental.pallas import tpu as pltpu
from jax.sharding import PartitionSpec as P

AXES = ("blk", "grp")
MESH = pl.DeviceIdType.MESH
MIB = 1024 * 1024
F32, BF16, I32 = jnp.float32, jnp.bfloat16, jnp.int32

LANES = 256
HALVES = 2
BLOCKS = 16
STEPS = 4
ORDERS = (
    (0, 4, 3, 2, 1, 5), (1, 4, 5, 0, 2, 3), (2, 3, 4, 1, 0, 5), (3, 1, 2, 5, 4, 0),
    (4, 1, 0, 3, 2, 5), (5, 4, 3, 2, 0, 1), (0, 5, 2, 3, 1, 4), (1, 3, 4, 5, 0, 2),
    (2, 0, 4, 5, 3, 1), (3, 5, 1, 0, 4, 2), (4, 2, 1, 5, 0, 3), (5, 2, 0, 3, 4, 1),
    (0, 5, 1, 3, 2, 4), (1, 0, 5, 4, 2, 3), (2, 4, 0, 1, 3, 5), (3, 5, 2, 4, 0, 1),
)


def split_bf16(values):
    high = values.astype(BF16)
    low = (values - high.astype(F32)).astype(BF16)
    return high, low


def dot3(left, right_high, right_low):
    high, low = split_bf16(left)
    dot = functools.partial(jnp.dot, preferred_element_type=F32)
    return dot(high, right_high) + (dot(high, right_low) + dot(low, right_high))


def fourier_tables(pixels, order_count, width):
    coarse = pixels // width
    k1, m1 = np.meshgrid(np.arange(coarse), np.arange(coarse), indexing="ij")
    angle = 2.0 * math.pi * ((k1 * m1) % coarse) / coarse
    first = np.concatenate([np.cos(angle.T), -np.sin(angle.T)], axis=0)
    k2 = np.arange(width)[:, None]
    m = np.arange(order_count)[None, :]
    angle = 2.0 * math.pi * ((k2 * m) % pixels) / pixels
    cosine, sine = np.cos(angle) / math.sqrt(pixels), np.sin(angle) / math.sqrt(pixels)
    second = np.block([[cosine, -sine], [sine, cosine]]).astype(np.float32)
    high = second.astype(BF16)
    low = (second - high.astype(np.float32)).astype(BF16)
    return first.astype(np.float32), high, low


def position():
    blk, grp = lax.axis_index("blk"), lax.axis_index("grp")
    x, y = blk // 16, (blk // 4) % 4
    z = grp * 2 + (blk // 2) % 2
    return x, y, z, blk % 2


def device_at(x, y, z, core):
    return ((x * 4 + y) * 2 + z % 2) * 2 + core, z // 2


def moved(chip, gen):
    axis, kind = gen % 3, gen // 3
    out = []
    for i, c in enumerate(chip):
        other = jnp.where(kind == 0, c + 1 - 2 * (c % 2), 3 - c)
        out.append(jnp.where(axis == i, other, c))
    return tuple(out)


def look_up(values, index):
    total = jnp.int32(0)
    for i, value in enumerate(values):
        if value:
            total = total + jnp.where(index == i, jnp.int32(value), jnp.int32(0))
    return total


def row_slots():
    out = np.zeros((4, BLOCKS, 256), np.int32)
    for b, order in enumerate(ORDERS):
        for row in range(256):
            part, rel, j = row // 128, (row % 128) // 2, row % 2
            flips = [0, 0, 0]
            for k, gen in enumerate(order):
                if (rel >> (5 - k)) & 1:
                    flips[gen % 3] ^= 1 if gen // 3 == 0 else 3
            out[0, b, row] = flips[0] * 16 + flips[1] * 4 + flips[2]
            out[1, b, row] = part
            out[2, b, row] = (b % HALVES) * 2 + j
    return out[:3]


def spectral_values(rows, coarse, x_ref, first, high, low, order_count):
    columns = 2 * order_count
    m1 = lax.broadcasted_iota(I32, (1, coarse, columns), 1)
    col = lax.broadcasted_iota(I32, (1, coarse, columns), 2)
    keep = (col % coarse) == m1
    stages = []
    for b in range(rows):
        stage = jnp.dot(
            first,
            x_ref[b * coarse : (b + 1) * coarse, :],
            precision=lax.Precision.HIGHEST,
            preferred_element_type=F32,
        )
        stages.append(jnp.concatenate([stage[:coarse], stage[coarse:]], axis=1))
    full = dot3(jnp.concatenate(stages, axis=0), high, low)
    full = full.reshape(rows, coarse, columns)
    return jnp.sum(jnp.where(keep, full, 0.0), axis=1).astype(BF16)


def main_body(
    maps,
    cycles,
    orders,
    legendre_ref,
    sky_ref,
    first_ref,
    high_ref,
    low_ref,
    table_ref,
    owned_ref,
    harm_ref,
    spectra_ref,
    leg,
    sky,
    first_buf,
    high_buf,
    low_buf,
    hot,
    own,
    out_core,
    got,
    four,
    four_got,
    coefs,
    s1,
    r1,
    s2,
    r2,
    s3,
    r3,
    s4,
    r4,
    s5,
    r5,
    acc,
    power,
    power_got,
    column,
    column_got,
    leg_sem,
    in_sem,
    core_send,
    core_recv,
    four_sem,
    step_send,
    step_recv,
    last_send,
    last_recv,
    power_sem,
    column_sem,
):
    x, y, z, core = position()
    chip = (x, y, z)
    place = x * 4 + y
    member = ((z % 2) * 2 + core) * 2 + z // 2
    members = 8
    columns = power.shape[0]
    channels = 2 * maps
    tiles = legendre_ref.shape[2] // LANES

    def leg_copy(t):
        return pltpu.make_async_copy(
            legendre_ref.at[:, :, pl.ds(pl.multiple_of(t * LANES, LANES), LANES)], leg.at[t], leg_sem.at[t]
        )

    leg_copy(0).start()
    loads = [
        pltpu.make_async_copy(src, dst, in_sem.at[i])
        for i, (src, dst) in enumerate(
            [(sky_ref, sky), (first_ref, first_buf), (high_ref, high_buf), (low_ref, low_buf)]
        )
    ]
    for load in loads:
        load.start()
    for t in range(1, tiles):
        leg_copy(t).start()

    barrier = pltpu.get_barrier_semaphore()
    partner = device_at(x, y, z, 1 - core)
    near = [partner] + [device_at(*moved(chip, jnp.int32(g)), core) for g in range(6)]
    for device in near:
        pl.semaphore_signal(barrier, inc=1, device_id=device, device_id_type=MESH)

    def remote(src, dst, send, recv, device):
        return pltpu.make_async_remote_copy(
            src_ref=src, dst_ref=dst, send_sem=send, recv_sem=recv, device_id=device, device_id_type=MESH
        )

    def core_copy(b):
        return remote(out_core.at[b], got.at[b], core_send, core_recv.at[b], partner)

    def permute(b):
        t = b // HALVES
        lane = lax.broadcasted_iota(I32, (256, BLOCKS), 1)
        column = jnp.sum(jnp.where(lane == b, table_ref[...], 0), axis=1, keepdims=True)
        one_hot = jnp.where(column == lax.broadcasted_iota(I32, (256, orders), 1), 1.0, 0.0).astype(BF16)
        hot[b] = one_hot[:128]
        for r in range(cycles):
            picked = jnp.dot(one_hot, leg[t, r], preferred_element_type=F32).astype(BF16)
            own[b, r] = picked[:128]
            out_core[b, r] = picked[128:]

    leg_copy(0).wait()
    permute(0)
    pl.semaphore_wait(barrier, len(near))
    core_copy(0).start()
    permute(1)
    core_copy(1).start()

    for load in loads:
        load.wait()
    rows = maps * cycles
    coarse = sky.shape[0] // rows
    spectral = spectral_values(rows, coarse, sky, first_buf[...], high_buf[...], low_buf[...], orders)
    out_row = lax.broadcasted_iota(I32, (cycles * channels, rows), 0)
    in_row = lax.broadcasted_iota(I32, (cycles * channels, rows), 1)
    value = jnp.zeros((cycles * channels, orders), F32)
    for q in range(2):
        wanted = (in_row % cycles) * channels + 2 * (in_row // cycles) + q
        pick = jnp.where(out_row == wanted, 1.0, 0.0).astype(BF16)
        value = value + jnp.dot(pick, spectral[:, q * orders : (q + 1) * orders], preferred_element_type=F32)
    four[...] = value.astype(BF16)
    four_copy = remote(four, four_got, four_sem.at[0], four_sem.at[1], partner)
    four_copy.start()

    def coefficients(b):
        every = jnp.concatenate([four[...], four_got[...]], axis=0)
        coefs[b] = lax.dot_general(
            every, hot[b], (((1,), (1,)), ((), ())), preferred_element_type=F32
        )

    def partial(b, g):
        lane = lax.broadcasted_iota(I32, (channels, 128), 1) // 32
        sides = []
        for side in range(2):
            total = jnp.zeros((channels, 128), F32)
            for q in range(4):
                r = side * 4 + q
                piece = coefs[b, r * channels : (r + 1) * channels, :]
                shift = (32 * (q - g)) % 128
                piece = pltpu.roll(piece, shift, 1) if shift else piece
                total = jnp.where(lane == q, piece, total)
            sides.append(total)
        line = jnp.concatenate(sides, axis=1)
        wide = jnp.broadcast_to(line[None], (32, channels, 256)).reshape(256, 256)
        row = lax.broadcasted_iota(I32, (256, 256), 0) // channels
        col = lax.broadcasted_iota(I32, (256, 256), 1) % 32
        left = jnp.where(row == col, wide, 0.0).astype(BF16)
        right = jnp.concatenate(
            [ref[b, r, 32 * g : 32 * (g + 1), :] for ref in (own, got) for r in range(cycles)], axis=0
        )
        return jnp.dot(left, right, preferred_element_type=F32)

    senders, receivers = (s1, s2, s3, s4), (r1, r2, r3, r4)

    def step_copy(k, b):
        gen = look_up([order[k] for order in ORDERS], b)
        device = device_at(*moved(chip, gen), core)
        return remote(senders[k].at[b], receivers[k].at[b], step_send.at[k], step_recv.at[k, b], device)

    def first_step(b):
        core_copy(b).wait_recv()
        coefficients(b)
        for g in (2, 3):
            s1[b, (g - 2) * 256 : (g - 1) * 256] = partial(b, g).astype(BF16)
        step_copy(0, b).start()

    four_copy.wait_recv()

    def front(t, carry):
        @pl.when(t + 1 < tiles)
        def _():
            leg_copy(t + 1).wait()
            for h in range(HALVES):
                b = HALVES * (t + 1) + h
                permute(b)
                core_copy(b).start()

        for h in range(HALVES):
            first_step(HALVES * t + h)
        return carry

    lax.fori_loop(0, tiles, front, 0)

    def second(b, carry):
        low = partial(b, 0)
        high = partial(b, 1)
        step_copy(0, b).wait_recv()
        s2[b] = (high + r1[b, 256:512].astype(F32)).astype(BF16)
        step_copy(1, b).start()
        acc[b] = low + r1[b, 0:256].astype(F32)
        return carry

    lax.fori_loop(0, BLOCKS, second, 0)

    def third(b, carry):
        step_copy(1, b).wait_recv()
        s3[b] = (acc[b, 128:256] + r2[b, 128:256].astype(F32)).astype(BF16)
        step_copy(2, b).start()
        acc[b, 0:128] = acc[b, 0:128] + r2[b, 0:128].astype(F32)
        return carry

    lax.fori_loop(0, BLOCKS, third, 0)

    def fourth(b, carry):
        step_copy(2, b).wait_recv()
        s4[b] = (acc[b, 64:128] + r3[b, 64:128].astype(F32)).astype(BF16)
        step_copy(3, b).start()
        acc[b, 0:64] = acc[b, 0:64] + r3[b, 0:64].astype(F32)
        return carry

    lax.fori_loop(0, BLOCKS, fourth, 0)

    def last_copies(b):
        gens = [look_up([order[k] for order in ORDERS], b) for k in (4, 5)]
        to = [moved(chip, gens[1]), moved(chip, gens[0])]
        to.append(moved(to[0], gens[0]))
        return [
            remote(s5.at[b, i], r5.at[b, i], last_send.at[i], last_recv.at[b, i], device_at(*where, core))
            for i, where in enumerate(to)
        ]

    def fifth(b, carry):
        step_copy(3, b).wait_recv()
        total = acc[b, 16:64] + r4[b, 16:64].astype(F32)
        for i in range(3):
            s5[b, i] = total[16 * i : 16 * (i + 1)].astype(BF16)
        for copy in last_copies(b):
            copy.start()
        acc[b, 0:16] = acc[b, 0:16] + r4[b, 0:16].astype(F32)
        return carry

    lax.fori_loop(0, BLOCKS, fifth, 0)

    def power_copy(c):
        device = device_at(c // 4, c % 4, z, core)
        return remote(power.at[c], power_got.at[place], power_sem.at[0], power_sem.at[1], device)

    def column_copy(n):
        there = (n % 2) * 2 + n // 4
        device = device_at(x, y, there, (n // 2) % 2)
        return remote(column, column_got.at[member], column_sem.at[0], column_sem.at[1], device)

    def finish(t, carry):
        start = pl.multiple_of(t * LANES, LANES)
        ell = start + lax.broadcasted_iota(I32, (2 * channels, LANES), 1)
        total = [None] * maps
        for h in range(HALVES):
            b = HALVES * t + h
            for copy in last_copies(b):
                copy.wait_recv()
            value = acc[b, 0:16]
            for i in range(3):
                value = value + r5[b, i].astype(F32)
            order = owned_ref[16 * h : 16 * (h + 1), 0:1]
            value = jnp.where(ell >= order, value, 0.0)
            for s in range(2):
                for a in range(maps):
                    row = s * channels + 2 * a
                    harm_ref[2 * h + s, a, :, pl.ds(start, LANES)] = value[row : row + 2]
            weighted = jnp.where(order == 0, value, 2.0 * value)
            for s in range(2):
                mode = value[s * channels : (s + 1) * channels]
                heavy = weighted[s * channels : (s + 1) * channels]
                for k in range(maps // 2 + 1):
                    turned = mode if k == 0 else jnp.concatenate([mode[2 * k :], mode[: 2 * k]], axis=0)
                    term = heavy * turned
                    total[k] = term if total[k] is None else total[k] + term
        lines = []
        for i in range(maps):
            for j in range(i, maps):
                k, a = (j - i, i) if j - i <= maps // 2 else (maps - (j - i), j)
                lines.append(total[k][2 * a : 2 * a + 1] + total[k][2 * a + 1 : 2 * a + 2])
        lines.append(jnp.zeros((power.shape[1] - len(lines), LANES), F32))
        block = jnp.concatenate(lines, axis=0)
        for half in range(LANES // 128):
            c = (LANES // 128) * t + half
            power[c] = block[:, 128 * half : 128 * (half + 1)]

            @pl.when(c != place)
            def _():
                power_copy(c).start()

        return carry

    lax.fori_loop(0, tiles, finish, 0)

    others = columns - 1
    remote(
        power.at[0:others], power_got.at[0:others], power_sem.at[0], power_sem.at[1], partner
    ).wait_recv()
    power_got[place] = power[place]
    total = power_got[0]
    for c in range(1, columns):
        total = total + power_got[c]
    column[...] = total
    for n in range(members):

        @pl.when(n != member)
        def _():
            column_copy(n).start()

    others = members - 1
    whole = remote(
        column_got.at[0:others], column_got.at[0:others], column_sem.at[0], column_sem.at[1], partner
    )
    whole.wait_recv()
    column_got[member] = column[...]
    total = column_got[0]
    for n in range(1, members):
        total = total + column_got[n]
    share = spectra_ref.shape[1]
    ell = place * 128 + lax.broadcasted_iota(I32, total.shape, 1)
    total = total / (2 * ell + 1).astype(F32)
    total = pltpu.roll(total, (128 - share * member) % 128, 1)
    spectra_ref[...] = total[: spectra_ref.shape[0], :share]

    whole.wait_send()
    remote(power.at[0 : columns - 1], power.at[0 : columns - 1], power_sem.at[0], power_sem.at[1], partner).wait_send()
    remote(out_core, got, core_send, core_recv.at[0], partner).wait_send()
    four_copy.wait_send()
    for k in range(STEPS):
        remote(senders[k], receivers[k], step_send.at[k], step_recv.at[k, 0], partner).wait_send()
    for i in range(3):
        remote(s5.at[:, i], r5.at[:, i], last_send.at[i], last_recv.at[0, i], partner).wait_send()


def main_call(devices, sky_maps, legendre, table, owned):
    maps, cycles, pixels = sky_maps.shape
    _, orders, ells = legendre.shape
    width = 128
    coarse = pixels // width
    rows = maps * cycles
    channels = 2 * maps
    tiles = ells // LANES
    pairs = maps * (maps + 1) // 2
    first, high, low = fourier_tables(pixels, orders, width)
    hbm = pl.BlockSpec(memory_space=pl.ANY)
    vmem = pl.BlockSpec(memory_space=pltpu.VMEM)

    def steps(rows_of):
        return [pltpu.VMEM((BLOCKS, n, LANES), BF16) for n in rows_of for _ in range(2)]

    return pl.pallas_call(
        functools.partial(main_body, maps, cycles, orders),
        out_shape=[
            jax.ShapeDtypeStruct((4, maps, 2, ells), F32),
            jax.ShapeDtypeStruct((pairs, ells // devices), F32),
        ],
        in_specs=[hbm] * 5 + [vmem] * 2,
        out_specs=[vmem] * 2,
        scratch_shapes=[
            pltpu.VMEM((tiles, cycles, orders, LANES), BF16),
            pltpu.VMEM((rows * coarse, width), F32),
            pltpu.VMEM(first.shape, F32),
            pltpu.VMEM(high.shape, BF16),
            pltpu.VMEM(low.shape, BF16),
            pltpu.VMEM((BLOCKS, 128, orders), BF16),
            pltpu.VMEM((BLOCKS, cycles, 128, LANES), BF16),
            pltpu.VMEM((BLOCKS, cycles, 128, LANES), BF16),
            pltpu.VMEM((BLOCKS, cycles, 128, LANES), BF16),
            pltpu.VMEM((cycles * channels, orders), BF16),
            pltpu.VMEM((cycles * channels, orders), BF16),
            pltpu.VMEM((BLOCKS, 2 * cycles * channels, 128), F32),
            *steps((512, 256, 128, 64)),
            pltpu.VMEM((BLOCKS, 3, 16, LANES), BF16),
            pltpu.VMEM((BLOCKS, 3, 16, LANES), BF16),
            pltpu.VMEM((BLOCKS, 256, LANES), F32),
            pltpu.VMEM((ells // 128, 16, 128), F32),
            pltpu.VMEM((ells // 128, 16, 128), F32),
            pltpu.VMEM((16, 128), F32),
            pltpu.VMEM((8, 16, 128), F32),
            pltpu.SemaphoreType.DMA((tiles,)),
            pltpu.SemaphoreType.DMA((4,)),
            pltpu.SemaphoreType.DMA,
            pltpu.SemaphoreType.DMA((BLOCKS,)),
            pltpu.SemaphoreType.DMA((2,)),
            pltpu.SemaphoreType.DMA((STEPS,)),
            pltpu.SemaphoreType.DMA((STEPS, BLOCKS)),
            pltpu.SemaphoreType.DMA((3,)),
            pltpu.SemaphoreType.DMA((BLOCKS, 3)),
            pltpu.SemaphoreType.DMA((2,)),
            pltpu.SemaphoreType.DMA((2,)),
        ],
        compiler_params=pltpu.CompilerParams(
            collective_id=0, has_side_effects=True, vmem_limit_bytes=58 * MIB
        ),
        cost_estimate=pl.CostEstimate(flops=10_000_000_000, bytes_accessed=16 * MIB, transcendentals=0),
    )(
        legendre,
        sky_maps.reshape(rows * coarse, width),
        jnp.asarray(first),
        jnp.asarray(high),
        jnp.asarray(low),
        table,
        owned,
    )


def per_device(sky_maps, legendre, owner_table):
    maps = sky_maps.shape[0]
    _, order_count, _ = legendre.shape
    devices = lax.axis_size(AXES)
    own_count = order_count // devices
    channels = 2 * maps
    me = lax.axis_index(AXES)
    x, y, z, core = position()

    flips, parts, items = (jnp.asarray(v.T) for v in row_slots())
    chips = (x * 16 + y * 4 + z) ^ flips
    z_of = chips % 4
    device = (((chips // 4) * 2 + z_of % 2) * 2 + (core ^ parts)) * 2 + z_of // 2
    slot = device * own_count + items
    index = lax.iota(I32, order_count)
    table = jnp.sum(jnp.where(slot[:, :, None] == index, owner_table, 0), axis=2)

    owned = lax.dynamic_slice_in_dim(owner_table, me * own_count, own_count)
    owned = jnp.broadcast_to(owned[:, None, None], (own_count, channels, 128)).reshape(-1, 128)
    harmonics, spectra = main_call(devices, sky_maps, legendre, table, owned)
    return (harmonics, spectra)


def solution(mesh):
    return jax.shard_map(
        per_device,
        mesh=mesh,
        in_specs=(P(None, AXES, None), P(AXES, None, None), P()),
        out_specs=(P(AXES, None, None, None), P(None, AXES)),
        check_vma=False,
    )
```

profile of v0, /device:TPU:7, one launch (start us, length us, event | category | flops | bytes accessed | tf_op | source)
XLA Modules:
  0.0 80.8 jit_solution(9975232977743485616)
XLA Ops:
  0.7 0.8 dynamic_slice.3
  1.5 0.1 broadcast_in_dim.22
  1.5 0.1 broadcast_in_dim.23
  1.6 0.7 broadcast_in_dim.24.owned_ref
  2.3 1.3 %fusion.7 = s32[256,16]{1,0:T(8,128)S(1)} fusion(s32[256,16]{1,0:T(8,128)} %constant.113.clone, s32[256,16]{1,0:T(8,128)} %constant.111.clone, s32[256,16]{1,0:T(8,128)} %constant.112.clone, s32[]{:T(128)S(6)} %select_n.58, s32[]{:T(128)S(6)} %add.56), kind=kLoop, calls=%fused_computation.22 | loop fusion | flops 196608 | bytes 65544 | tf_op jit(solution)/shard_map/add | solution.py:531
  3.6 7.1 %select_reduce_fusion.table_ref = s32[256,16]{1,0:T(8,128)} fusion(s32[512]{0:T(512)} %param.11, s32[256,16]{1,0:T(8,128)S(1)} %fusion.7), kind=kLoop, calls=%fused_computation | loop fusion | flops 6287360 | bytes 34816 | tf_op jit(solution)/shard_map/reduce_sum | solution.py:533
  10.7 1.8 %reshape.11.sky_ref = f32[512,128]{1,0:T(8,128)} reshape(f32[4,4,4096]{2,1,0:T(4,128)} %param.9) | data formatting | bytes 524288 | tf_op jit(solution)/shard_map/reshape | solution.py:509
  12.5 65.3 %shard_map.104 = (f32[4,4,2,2048]{3,2,1,0:T(2,128)}, f32[10,16]{1,0:T(8,128)}) custom-call(bf16[4,512,2048]{2,1,0:T(8,128)(2,1)} %legendre_ref.1, f32[512,128]{1,0:T(8,128)} %reshape.11.sky_ref, f32[64,32]{1,0:T(8,128)} %constant.114.clone.first_ref, bf16[256,1024]{1,0:T(8,128)(2,1)} %constant.115.clone.high_ref, bf16[256,1024]{1,0:T(8,128)(2,1)} %constant.116.clone.low_ref, ...), custom_call_target="tpu_custom_call" | custom-call | flops 10000000000 | bytes 16777216 | tf_op jit(solution)/shard_map/pallas_call | solution.py:462
  77.8 1.7 %copy.13 = f32[4,4,2,2048]{3,2,1,0:T(2,128)} copy(f32[4,4,2,2048]{3,2,1,0:T(2,128)} %get-tuple-element.4) | data formatting | bytes 524288
  79.5 1.3 %copy.14 = f32[10,16]{1,0:T(8,128)} copy(f32[10,16]{1,0:T(8,128)} %get-tuple-element.5) | data formatting | bytes 1280
where the time goes:
time: 81.1 us; the launch traced here: 80.8 us
  Pallas kernels  65.3 us (81%)
  other arithmetic  8.37 us (10%)
  local copies, waits for them, and re-layouts  6.39 us (8%)
    pallas_call x1, Pallas kernels, main_call(): pl.pallas_call(functools.partial(main_body, maps, cycles, orders), out_sh...  65.3 us
    reduce_sum x1, other arithmetic, per_device(): jnp.sum(jnp.where(slot[:, :, None] == index, owner_table, 0), axis=2)  7.07 us
    unnamed x2, local copies, waits for them, and re-layouts  2.97 us
    reshape x1, local copies, waits for them, and re-layouts, main_call(): sky_maps.reshape(rows * coarse, width)  1.83 us

commit v1 on v0

--- a/solution.py
+++ b/solution.py
@@ -81,8 +81,8 @@
     return total
 
 
-def row_slots():
-    out = np.zeros((4, BLOCKS, 256), np.int32)
+def row_flips():
+    out = np.zeros((2 * BLOCKS, 128), np.int32)
     for b, order in enumerate(ORDERS):
         for row in range(256):
             part, rel, j = row // 128, (row % 128) // 2, row % 2
@@ -90,13 +90,12 @@
             for k, gen in enumerate(order):
                 if (rel >> (5 - k)) & 1:
                     flips[gen % 3] ^= 1 if gen // 3 == 0 else 3
-            out[0, b, row] = flips[0] * 16 + flips[1] * 4 + flips[2]
-            out[1, b, row] = part
-            out[2, b, row] = (b % HALVES) * 2 + j
-    return out[:3]
-
-
-def spectral_values(rows, coarse, x_ref, first, high, low, order_count):
+            device = ((flips[0] * 4 + flips[1]) * 2 + flips[2] % 2) * 4 + part * 2 + flips[2] // 2
+            out[2 * b + part, row % 128] = device * 4 + (b % HALVES) * 2 + j
+    return out
+
+
+def spectral_values(rows, cycles, coarse, x_ref, first, high, low, order_count):
     columns = 2 * order_count
     m1 = lax.broadcasted_iota(I32, (1, coarse, columns), 1)
     col = lax.broadcasted_iota(I32, (1, coarse, columns), 2)
@@ -105,7 +104,7 @@
     for b in range(rows):
         stage = jnp.dot(
             first,
-            x_ref[b * coarse : (b + 1) * coarse, :],
+            x_ref[b // cycles, b % cycles],
             precision=lax.Precision.HIGHEST,
             preferred_element_type=F32,
         )
@@ -124,8 +123,9 @@
     first_ref,
     high_ref,
     low_ref,
+    flips_ref,
     table_ref,
-    owned_ref,
+    owner_ref,
     harm_ref,
     spectra_ref,
     leg,
@@ -133,6 +133,7 @@
     first_buf,
     high_buf,
     low_buf,
+    lines,
     hot,
     own,
     out_core,
@@ -182,14 +183,21 @@
         )
 
     leg_copy(0).start()
+    coarse = sky.shape[2]
+
+    def sky_copy(k, carry):
+        lanes = pl.ds(pl.multiple_of(k * 128, 128), 128)
+        pltpu.make_async_copy(sky_ref.at[:, :, lanes], sky.at[:, :, k, :], in_sem.at[0]).start()
+        return carry
+
     loads = [
-        pltpu.make_async_copy(src, dst, in_sem.at[i])
-        for i, (src, dst) in enumerate(
-            [(sky_ref, sky), (first_ref, first_buf), (high_ref, high_buf), (low_ref, low_buf)]
-        )
+        pltpu.make_async_copy(src, dst, in_sem.at[i + 1])
+        for i, (src, dst) in enumerate([(first_ref, first_buf), (high_ref, high_buf), (low_ref, low_buf)])
     ]
+    lax.fori_loop(0, coarse, sky_copy, 0)
     for load in loads:
         load.start()
+    loads.append(pltpu.make_async_copy(sky, sky, in_sem.at[0]))
     for t in range(1, tiles):
         leg_copy(t).start()
 
@@ -209,8 +217,7 @@
 
     def permute(b):
         t = b // HALVES
-        lane = lax.broadcasted_iota(I32, (256, BLOCKS), 1)
-        column = jnp.sum(jnp.where(lane == b, table_ref[...], 0), axis=1, keepdims=True)
+        column = jnp.transpose(lines[b])[:, 0:1].astype(I32)
         one_hot = jnp.where(column == lax.broadcasted_iota(I32, (256, orders), 1), 1.0, 0.0).astype(BF16)
         hot[b] = one_hot[:128]
         for r in range(cycles):
@@ -218,6 +225,16 @@
             own[b, r] = picked[:128]
             out_core[b, r] = picked[128:]
 
+    base = ((place * 2 + z % 2) * 4 + core * 2 + z // 2) * 4
+    digits = jnp.concatenate([table_ref[...] >> 4, table_ref[...] & 15], axis=0).astype(F32).astype(BF16)
+    for b in range(BLOCKS):
+        slot = jnp.concatenate([flips_ref[2 * b + i : 2 * b + i + 1, :] for i in range(2)], axis=1) ^ base
+        spot = jnp.where(lax.broadcasted_iota(I32, (128, 256), 0) == (slot & 127), 1.0, 0.0).astype(BF16)
+        found = jnp.dot(digits, spot, preferred_element_type=F32)
+        found = found[0:4] * 16.0 + found[4:8]
+        found = jnp.where(lax.broadcasted_iota(I32, (4, 256), 0) == (slot >> 7), found, 0.0)
+        lines[b] = jnp.broadcast_to(jnp.sum(found, axis=0, keepdims=True), (8, 256))
+
     leg_copy(0).wait()
     permute(0)
     pl.semaphore_wait(barrier, len(near))
@@ -228,8 +245,7 @@
     for load in loads:
         load.wait()
     rows = maps * cycles
-    coarse = sky.shape[0] // rows
-    spectral = spectral_values(rows, coarse, sky, first_buf[...], high_buf[...], low_buf[...], orders)
+    spectral = spectral_values(rows, cycles, coarse, sky, first_buf[...], high_buf[...], low_buf[...], orders)
     out_row = lax.broadcasted_iota(I32, (cycles * channels, rows), 0)
     in_row = lax.broadcasted_iota(I32, (cycles * channels, rows), 1)
     value = jnp.zeros((cycles * channels, orders), F32)
@@ -370,7 +386,8 @@
             value = acc[b, 0:16]
             for i in range(3):
                 value = value + r5[b, i].astype(F32)
-            order = owned_ref[16 * h : 16 * (h + 1), 0:1]
+            pair = [owner_ref[base + 2 * h + s] for s in range(2)]
+            order = jnp.where(lax.broadcasted_iota(I32, (2 * channels, 1), 0) < channels, pair[0], pair[1])
             value = jnp.where(ell >= order, value, 0.0)
             for s in range(2):
                 for a in range(maps):
@@ -443,12 +460,11 @@
         remote(s5.at[:, i], r5.at[:, i], last_send.at[i], last_recv.at[0, i], partner).wait_send()
 
 
-def main_call(devices, sky_maps, legendre, table, owned):
+def main_call(devices, sky_maps, legendre, owner_table):
     maps, cycles, pixels = sky_maps.shape
     _, orders, ells = legendre.shape
     width = 128
     coarse = pixels // width
-    rows = maps * cycles
     channels = 2 * maps
     tiles = ells // LANES
     pairs = maps * (maps + 1) // 2
@@ -465,14 +481,15 @@
             jax.ShapeDtypeStruct((4, maps, 2, ells), F32),
             jax.ShapeDtypeStruct((pairs, ells // devices), F32),
         ],
-        in_specs=[hbm] * 5 + [vmem] * 2,
+        in_specs=[hbm] * 5 + [vmem] * 2 + [pl.BlockSpec(memory_space=pltpu.SMEM)],
         out_specs=[vmem] * 2,
         scratch_shapes=[
             pltpu.VMEM((tiles, cycles, orders, LANES), BF16),
-            pltpu.VMEM((rows * coarse, width), F32),
+            pltpu.VMEM((maps, cycles, coarse, width), F32),
             pltpu.VMEM(first.shape, F32),
             pltpu.VMEM(high.shape, BF16),
             pltpu.VMEM(low.shape, BF16),
+            pltpu.VMEM((BLOCKS, 8, 256), F32),
             pltpu.VMEM((BLOCKS, 128, orders), BF16),
             pltpu.VMEM((BLOCKS, cycles, 128, LANES), BF16),
             pltpu.VMEM((BLOCKS, cycles, 128, LANES), BF16),
@@ -506,35 +523,19 @@
         cost_estimate=pl.CostEstimate(flops=10_000_000_000, bytes_accessed=16 * MIB, transcendentals=0),
     )(
         legendre,
-        sky_maps.reshape(rows * coarse, width),
+        sky_maps,
         jnp.asarray(first),
         jnp.asarray(high),
         jnp.asarray(low),
-        table,
-        owned,
+        jnp.asarray(row_flips()),
+        owner_table.reshape(4, 128),
+        owner_table,
     )
 
 
 def per_device(sky_maps, legendre, owner_table):
-    maps = sky_maps.shape[0]
-    _, order_count, _ = legendre.shape
     devices = lax.axis_size(AXES)
-    own_count = order_count // devices
-    channels = 2 * maps
-    me = lax.axis_index(AXES)
-    x, y, z, core = position()
-
-    flips, parts, items = (jnp.asarray(v.T) for v in row_slots())
-    chips = (x * 16 + y * 4 + z) ^ flips
-    z_of = chips % 4
-    device = (((chips // 4) * 2 + z_of % 2) * 2 + (core ^ parts)) * 2 + z_of // 2
-    slot = device * own_count + items
-    index = lax.iota(I32, order_count)
-    table = jnp.sum(jnp.where(slot[:, :, None] == index, owner_table, 0), axis=2)
-
-    owned = lax.dynamic_slice_in_dim(owner_table, me * own_count, own_count)
-    owned = jnp.broadcast_to(owned[:, None, None], (own_count, channels, 128)).reshape(-1, 128)
-    harmonics, spectra = main_call(devices, sky_maps, legendre, table, owned)
+    harmonics, spectra = main_call(devices, sky_maps, legendre, owner_table)
     return (harmonics, spectra)
 
 

time: 81.1 us -> 70.4 us (0.87)
  other arithmetic: 8.37 us -> 0 us
  local copies, waits for them, and re-layouts: 6.39 us -> 2.97 us
  Pallas kernels: 65.3 us -> 66.5 us
    reduce_sum x1 -> x0, other arithmetic: 7.07 us -> none  [per_device(): jnp.sum(jnp.where(slot[:, :, None] == index, owner_table, 0), axis=2)]
    reshape x1 -> x0, local copies, waits for them, and re-layouts: 1.83 us -> none  [main_call(): sky_maps.reshape(rows * coarse, width)]
    add x1 -> x0, other arithmetic: 1.3 us -> none  [per_device(): slot = device * own_count + items]
    pallas_call x1, Pallas kernels: 65.3 us -> 66.5 us  [main_call(): pl.pallas_call(functools.partial(main_body, maps, cycles, orders), out_sh...]
    broadcast_in_dim x3 -> x0, local copies, waits for them, and re-layouts: 0.83 us -> none  [per_device(): jnp.broadcast_to(owned[:, None, None], (own_count, channels, 128))]
where the time goes in v1:
time: 70.4 us; the launch traced here: 70.1 us
  Pallas kernels  66.5 us (94%)
  local copies, waits for them, and re-layouts  2.97 us (4%)
    pallas_call x1, Pallas kernels, main_call(): pl.pallas_call(functools.partial(main_body, maps, cycles, orders), out_sh...  66.5 us
    unnamed x2, local copies, waits for them, and re-layouts  2.97 us

profile of v1, /device:TPU:7, one launch (start us, length us, event | category | flops | bytes accessed | tf_op | source)
XLA Modules:
  0.0 70.1 jit_solution(2921774771270286760)
XLA Ops:
  0.6 66.5 %shard_map.86 = (f32[4,4,2,2048]{3,2,1,0:T(2,128)}, f32[10,16]{1,0:T(8,128)}) custom-call(bf16[4,512,2048]{2,1,0:T(8,128)(2,1)} %legendre_ref.1, f32[4,4,4096]{2,1,0:T(4,128)} %sky_ref.1, f32[64,32]{1,0:T(8,128)} %constant.8.clone.first_ref, bf16[256,1024]{1,0:T(8,128)(2,1)} %constant.9.clone.high_ref, bf16[256,1024]{1,0:T(8,128)(2,1)} %constant.10.clone.low_ref, ...), custom_call_target="tpu_custom_call" | custom-call | flops 10000000000 | bytes 16777216 | tf_op jit(solution)/shard_map/pallas_call | solution.py:478
  67.2 1.7 %copy.11 = f32[4,4,2,2048]{3,2,1,0:T(2,128)} copy(f32[4,4,2,2048]{3,2,1,0:T(2,128)} %get-tuple-element.4) | data formatting | bytes 524288
  68.8 1.3 %copy.12 = f32[10,16]{1,0:T(8,128)} copy(f32[10,16]{1,0:T(8,128)} %get-tuple-element.5) | data formatting | bytes 1280

commit v2 on v1

--- a/solution.py
+++ b/solution.py
@@ -50,7 +50,10 @@
     second = np.block([[cosine, -sine], [sine, cosine]]).astype(np.float32)
     high = second.astype(BF16)
     low = (second - high.astype(np.float32)).astype(BF16)
-    return first.astype(np.float32), high, low
+    first = first.astype(np.float32)
+    first_high = first.astype(BF16)
+    first_low = (first - first_high.astype(np.float32)).astype(BF16)
+    return np.stack([first_high, first_low]), high, low
 
 
 def position():
@@ -68,6 +71,9 @@
     axis, kind = gen % 3, gen // 3
     out = []
     for i, c in enumerate(chip):
+        if isinstance(gen, int):
+            out.append((c + 1 - 2 * (c % 2) if kind == 0 else 3 - c) if axis == i else c)
+            continue
         other = jnp.where(kind == 0, c + 1 - 2 * (c % 2), 3 - c)
         out.append(jnp.where(axis == i, other, c))
     return tuple(out)
@@ -82,36 +88,33 @@
 
 
 def row_flips():
-    out = np.zeros((2 * BLOCKS, 128), np.int32)
-    for b, order in enumerate(ORDERS):
-        for row in range(256):
-            part, rel, j = row // 128, (row % 128) // 2, row % 2
-            flips = [0, 0, 0]
-            for k, gen in enumerate(order):
-                if (rel >> (5 - k)) & 1:
-                    flips[gen % 3] ^= 1 if gen // 3 == 0 else 3
-            device = ((flips[0] * 4 + flips[1]) * 2 + flips[2] % 2) * 4 + part * 2 + flips[2] // 2
-            out[2 * b + part, row % 128] = device * 4 + (b % HALVES) * 2 + j
-    return out
-
-
-def spectral_values(rows, cycles, coarse, x_ref, first, high, low, order_count):
-    columns = 2 * order_count
+    out = np.zeros((2, BLOCKS // HALVES, HALVES, 2, 32, 2), np.int32)
+    for half, t, h, part, low, j in np.ndindex(*out.shape):
+        flips = [0, 0, 0]
+        for k, gen in enumerate(ORDERS[HALVES * t + h]):
+            if ((half * 32 + low) >> (5 - k)) & 1:
+                flips[gen % 3] ^= 1 if gen // 3 == 0 else 3
+        device = ((flips[0] * 4 + flips[1]) * 2 + flips[2] % 2) * 4 + part * 2 + flips[2] // 2
+        out[half, t, h, part, low, j] = device * 4 + h * 2 + j
+    return out.reshape(-1, 256)
+
+
+def spectral_values(x_ref, first, high, low):
+    maps, cycles, coarse, width = x_ref.shape
+    rows = maps * cycles
+    columns = high.shape[1]
+    x_high, x_low = split_bf16(jnp.concatenate([x_ref[i // cycles, i % cycles] for i in range(rows)], axis=1))
+    dot = functools.partial(jnp.dot, preferred_element_type=F32)
+    stage = dot(first[0], x_high) + (dot(first[0], x_low) + dot(first[1], x_high))
+    stages = []
+    for i in range(rows):
+        piece = stage[:, i * width : (i + 1) * width]
+        stages.append(jnp.concatenate([piece[:coarse], piece[coarse:]], axis=1))
+    full = dot3(jnp.concatenate(stages, axis=0), high, low)
     m1 = lax.broadcasted_iota(I32, (1, coarse, columns), 1)
     col = lax.broadcasted_iota(I32, (1, coarse, columns), 2)
-    keep = (col % coarse) == m1
-    stages = []
-    for b in range(rows):
-        stage = jnp.dot(
-            first,
-            x_ref[b // cycles, b % cycles],
-            precision=lax.Precision.HIGHEST,
-            preferred_element_type=F32,
-        )
-        stages.append(jnp.concatenate([stage[:coarse], stage[coarse:]], axis=1))
-    full = dot3(jnp.concatenate(stages, axis=0), high, low)
-    full = full.reshape(rows, coarse, columns)
-    return jnp.sum(jnp.where(keep, full, 0.0), axis=1).astype(BF16)
+    full = jnp.where((col % coarse) == m1, full.reshape(rows, coarse, columns), 0.0)
+    return jnp.sum(full, axis=1).astype(BF16)
 
 
 def main_body(
@@ -140,7 +143,6 @@
     got,
     four,
     four_got,
-    coefs,
     s1,
     r1,
     s2,
@@ -203,7 +205,8 @@
 
     barrier = pltpu.get_barrier_semaphore()
     partner = device_at(x, y, z, 1 - core)
-    near = [partner] + [device_at(*moved(chip, jnp.int32(g)), core) for g in range(6)]
+    across = [device_at(*moved(chip, g), core) for g in range(6)]
+    near = [partner] + across
     for device in near:
         pl.semaphore_signal(barrier, inc=1, device_id=device, device_id_type=MESH)
 
@@ -212,40 +215,38 @@
             src_ref=src, dst_ref=dst, send_sem=send, recv_sem=recv, device_id=device, device_id_type=MESH
         )
 
-    def core_copy(b):
-        return remote(out_core.at[b], got.at[b], core_send, core_recv.at[b], partner)
-
-    def permute(b):
-        t = b // HALVES
-        column = jnp.transpose(lines[b])[:, 0:1].astype(I32)
-        one_hot = jnp.where(column == lax.broadcasted_iota(I32, (256, orders), 1), 1.0, 0.0).astype(BF16)
-        hot[b] = one_hot[:128]
+    def core_copy(half, t):
+        return remote(out_core.at[half, t], got.at[half, t], core_send, core_recv.at[half, t], partner)
+
+    def make_hot(half, t):
+        column = jnp.transpose(lines[half * tiles + t])[:, 0:1].astype(I32)
+        lane = lax.broadcasted_iota(I32, (256, orders), 1)
+        hot[half, t] = jnp.where(column == lane, 1.0, 0.0).astype(BF16)
+
+    def permute(half, t):
+        one_hot = hot[half, t]
         for r in range(cycles):
             picked = jnp.dot(one_hot, leg[t, r], preferred_element_type=F32).astype(BF16)
-            own[b, r] = picked[:128]
-            out_core[b, r] = picked[128:]
+            for h in range(HALVES):
+                own[half, t, h, r] = picked[128 * h : 128 * h + 64]
+                out_core[half, t, h, r] = picked[128 * h + 64 : 128 * (h + 1)]
 
     base = ((place * 2 + z % 2) * 4 + core * 2 + z // 2) * 4
     digits = jnp.concatenate([table_ref[...] >> 4, table_ref[...] & 15], axis=0).astype(F32).astype(BF16)
-    for b in range(BLOCKS):
-        slot = jnp.concatenate([flips_ref[2 * b + i : 2 * b + i + 1, :] for i in range(2)], axis=1) ^ base
+    for i in range(2 * tiles):
+        slot = flips_ref[i : i + 1, :] ^ base
         spot = jnp.where(lax.broadcasted_iota(I32, (128, 256), 0) == (slot & 127), 1.0, 0.0).astype(BF16)
         found = jnp.dot(digits, spot, preferred_element_type=F32)
         found = found[0:4] * 16.0 + found[4:8]
         found = jnp.where(lax.broadcasted_iota(I32, (4, 256), 0) == (slot >> 7), found, 0.0)
-        lines[b] = jnp.broadcast_to(jnp.sum(found, axis=0, keepdims=True), (8, 256))
-
-    leg_copy(0).wait()
-    permute(0)
-    pl.semaphore_wait(barrier, len(near))
-    core_copy(0).start()
-    permute(1)
-    core_copy(1).start()
+        lines[i] = jnp.broadcast_to(jnp.sum(found, axis=0, keepdims=True), (8, 256))
+    for t in range(2):
+        make_hot(1, t)
 
     for load in loads:
         load.wait()
+    spectral = spectral_values(sky, first_buf, high_buf[...], low_buf[...])
     rows = maps * cycles
-    spectral = spectral_values(rows, cycles, coarse, sky, first_buf[...], high_buf[...], low_buf[...], orders)
     out_row = lax.broadcasted_iota(I32, (cycles * channels, rows), 0)
     in_row = lax.broadcasted_iota(I32, (cycles * channels, rows), 1)
     value = jnp.zeros((cycles * channels, orders), F32)
@@ -254,23 +255,26 @@
         pick = jnp.where(out_row == wanted, 1.0, 0.0).astype(BF16)
         value = value + jnp.dot(pick, spectral[:, q * orders : (q + 1) * orders], preferred_element_type=F32)
     four[...] = value.astype(BF16)
+    pl.semaphore_wait(barrier, len(near))
     four_copy = remote(four, four_got, four_sem.at[0], four_sem.at[1], partner)
     four_copy.start()
-
-    def coefficients(b):
+    leg_copy(0).wait()
+    permute(1, 0)
+    core_copy(1, 0).start()
+
+    def coefficients(half, t):
         every = jnp.concatenate([four[...], four_got[...]], axis=0)
-        coefs[b] = lax.dot_general(
-            every, hot[b], (((1,), (1,)), ((), ())), preferred_element_type=F32
-        )
-
-    def partial(b, g):
+        mine = jnp.concatenate([hot[half, t, 128 * h : 128 * h + 64, :] for h in range(HALVES)], axis=0)
+        return lax.dot_general(every, mine, (((1,), (1,)), ((), ())), preferred_element_type=F32)
+
+    def partial(half, t, coefs, g):
         lane = lax.broadcasted_iota(I32, (channels, 128), 1) // 32
         sides = []
         for side in range(2):
             total = jnp.zeros((channels, 128), F32)
             for q in range(4):
                 r = side * 4 + q
-                piece = coefs[b, r * channels : (r + 1) * channels, :]
+                piece = coefs[r * channels : (r + 1) * channels, :]
                 shift = (32 * (q - g)) % 128
                 piece = pltpu.roll(piece, shift, 1) if shift else piece
                 total = jnp.where(lane == q, piece, total)
@@ -280,24 +284,20 @@
         row = lax.broadcasted_iota(I32, (256, 256), 0) // channels
         col = lax.broadcasted_iota(I32, (256, 256), 1) % 32
         left = jnp.where(row == col, wide, 0.0).astype(BF16)
+        at = slice(32 * (g % 2), 32 * (g % 2) + 32)
         right = jnp.concatenate(
-            [ref[b, r, 32 * g : 32 * (g + 1), :] for ref in (own, got) for r in range(cycles)], axis=0
+            [ref[half, t, g // 2, r, at, :] for ref in (own, got) for r in range(cycles)], axis=0
         )
         return jnp.dot(left, right, preferred_element_type=F32)
 
     senders, receivers = (s1, s2, s3, s4), (r1, r2, r3, r4)
 
     def step_copy(k, b):
-        gen = look_up([order[k] for order in ORDERS], b)
-        device = device_at(*moved(chip, gen), core)
+        if isinstance(b, int):
+            device = across[ORDERS[b][k]]
+        else:
+            device = device_at(*moved(chip, look_up([order[k] for order in ORDERS], b)), core)
         return remote(senders[k].at[b], receivers[k].at[b], step_send.at[k], step_recv.at[k, b], device)
-
-    def first_step(b):
-        core_copy(b).wait_recv()
-        coefficients(b)
-        for g in (2, 3):
-            s1[b, (g - 2) * 256 : (g - 1) * 256] = partial(b, g).astype(BF16)
-        step_copy(0, b).start()
 
     four_copy.wait_recv()
 
@@ -305,56 +305,63 @@
         @pl.when(t + 1 < tiles)
         def _():
             leg_copy(t + 1).wait()
-            for h in range(HALVES):
-                b = HALVES * (t + 1) + h
-                permute(b)
-                core_copy(b).start()
-
+            permute(1, t + 1)
+            core_copy(1, t + 1).start()
+
+        core_copy(1, t).wait_recv()
+        coefs = coefficients(1, t)
+        for g in range(4):
+            s1[HALVES * t + g // 2, (g % 2) * 256 : (g % 2 + 1) * 256] = partial(1, t, coefs, g).astype(BF16)
+        ahead = t + 2
+        make_hot(jnp.where(ahead < tiles, 1, 0), ahead % tiles)
         for h in range(HALVES):
-            first_step(HALVES * t + h)
+            step_copy(0, HALVES * t + h).start()
         return carry
 
     lax.fori_loop(0, tiles, front, 0)
 
-    def second(b, carry):
-        low = partial(b, 0)
-        high = partial(b, 1)
-        step_copy(0, b).wait_recv()
-        s2[b] = (high + r1[b, 256:512].astype(F32)).astype(BF16)
-        step_copy(1, b).start()
-        acc[b] = low + r1[b, 0:256].astype(F32)
+    permute(0, 0)
+    core_copy(0, 0).start()
+
+    def second(t, carry):
+        @pl.when(t + 1 < tiles)
+        def _():
+            permute(0, t + 1)
+            core_copy(0, t + 1).start()
+
+        core_copy(0, t).wait_recv()
+        coefs = coefficients(0, t)
+        for g in range(4):
+            acc[HALVES * t + g // 2, (g % 2) * 256 : (g % 2 + 1) * 256] = partial(0, t, coefs, g)
+        make_hot(0, (t + 2) % tiles)
+        for h in range(HALVES):
+            b = HALVES * t + h
+            step_copy(0, b).wait_recv()
+            s2[b] = (acc[b, 256:512] + r1[b, 256:512].astype(F32)).astype(BF16)
+            step_copy(1, b).start()
+            acc[b, 0:256] = acc[b, 0:256] + r1[b, 0:256].astype(F32)
         return carry
 
-    lax.fori_loop(0, BLOCKS, second, 0)
-
-    def third(b, carry):
-        step_copy(1, b).wait_recv()
-        s3[b] = (acc[b, 128:256] + r2[b, 128:256].astype(F32)).astype(BF16)
-        step_copy(2, b).start()
-        acc[b, 0:128] = acc[b, 0:128] + r2[b, 0:128].astype(F32)
-        return carry
-
-    lax.fori_loop(0, BLOCKS, third, 0)
-
-    def fourth(b, carry):
-        step_copy(2, b).wait_recv()
-        s4[b] = (acc[b, 64:128] + r3[b, 64:128].astype(F32)).astype(BF16)
-        step_copy(3, b).start()
-        acc[b, 0:64] = acc[b, 0:64] + r3[b, 0:64].astype(F32)
-        return carry
-
-    lax.fori_loop(0, BLOCKS, fourth, 0)
+    lax.fori_loop(0, tiles, second, 0)
+
+    for k in (2, 3):
+        n = 512 >> k
+        for b in range(BLOCKS):
+            step_copy(k - 1, b).wait_recv()
+            got_ref = receivers[k - 1]
+            senders[k][b] = (acc[b, n : 2 * n] + got_ref[b, n : 2 * n].astype(F32)).astype(BF16)
+            step_copy(k, b).start()
+            acc[b, 0:n] = acc[b, 0:n] + got_ref[b, 0:n].astype(F32)
 
     def last_copies(b):
-        gens = [look_up([order[k] for order in ORDERS], b) for k in (4, 5)]
-        to = [moved(chip, gens[1]), moved(chip, gens[0])]
-        to.append(moved(to[0], gens[0]))
+        near, far = ORDERS[b][5], ORDERS[b][4]
+        to = [across[near], across[far], device_at(*moved(moved(chip, near), far), core)]
         return [
-            remote(s5.at[b, i], r5.at[b, i], last_send.at[i], last_recv.at[b, i], device_at(*where, core))
-            for i, where in enumerate(to)
+            remote(s5.at[b, i], r5.at[b, i], last_send.at[i], last_recv.at[b, i], device)
+            for i, device in enumerate(to)
         ]
 
-    def fifth(b, carry):
+    for b in range(BLOCKS):
         step_copy(3, b).wait_recv()
         total = acc[b, 16:64] + r4[b, 16:64].astype(F32)
         for i in range(3):
@@ -362,9 +369,6 @@
         for copy in last_copies(b):
             copy.start()
         acc[b, 0:16] = acc[b, 0:16] + r4[b, 0:16].astype(F32)
-        return carry
-
-    lax.fori_loop(0, BLOCKS, fifth, 0)
 
     def power_copy(c):
         device = device_at(c // 4, c % 4, z, core)
@@ -375,9 +379,9 @@
         device = device_at(x, y, there, (n // 2) % 2)
         return remote(column, column_got.at[member], column_sem.at[0], column_sem.at[1], device)
 
-    def finish(t, carry):
-        start = pl.multiple_of(t * LANES, LANES)
-        ell = start + lax.broadcasted_iota(I32, (2 * channels, LANES), 1)
+    def finish(t):
+        lanes = slice(t * LANES, (t + 1) * LANES)
+        ell = t * LANES + lax.broadcasted_iota(I32, (2 * channels, LANES), 1)
         total = [None] * maps
         for h in range(HALVES):
             b = HALVES * t + h
@@ -392,7 +396,7 @@
             for s in range(2):
                 for a in range(maps):
                     row = s * channels + 2 * a
-                    harm_ref[2 * h + s, a, :, pl.ds(start, LANES)] = value[row : row + 2]
+                    harm_ref[2 * h + s, a, :, lanes] = value[row : row + 2]
             weighted = jnp.where(order == 0, value, 2.0 * value)
             for s in range(2):
                 mode = value[s * channels : (s + 1) * channels]
@@ -401,13 +405,13 @@
                     turned = mode if k == 0 else jnp.concatenate([mode[2 * k :], mode[: 2 * k]], axis=0)
                     term = heavy * turned
                     total[k] = term if total[k] is None else total[k] + term
-        lines = []
+        rows = []
         for i in range(maps):
             for j in range(i, maps):
                 k, a = (j - i, i) if j - i <= maps // 2 else (maps - (j - i), j)
-                lines.append(total[k][2 * a : 2 * a + 1] + total[k][2 * a + 1 : 2 * a + 2])
-        lines.append(jnp.zeros((power.shape[1] - len(lines), LANES), F32))
-        block = jnp.concatenate(lines, axis=0)
+                rows.append(total[k][2 * a : 2 * a + 1] + total[k][2 * a + 1 : 2 * a + 2])
+        rows.append(jnp.zeros((power.shape[1] - len(rows), LANES), F32))
+        block = jnp.concatenate(rows, axis=0)
         for half in range(LANES // 128):
             c = (LANES // 128) * t + half
             power[c] = block[:, 128 * half : 128 * (half + 1)]
@@ -416,9 +420,8 @@
             def _():
                 power_copy(c).start()
 
-        return carry
-
-    lax.fori_loop(0, tiles, finish, 0)
+    for t in range(tiles):
+        finish(t)
 
     others = columns - 1
     remote(
@@ -451,8 +454,11 @@
     spectra_ref[...] = total[: spectra_ref.shape[0], :share]
 
     whole.wait_send()
-    remote(power.at[0 : columns - 1], power.at[0 : columns - 1], power_sem.at[0], power_sem.at[1], partner).wait_send()
-    remote(out_core, got, core_send, core_recv.at[0], partner).wait_send()
+    others = columns - 1
+    remote(
+        power.at[0:others], power_got.at[0:others], power_sem.at[0], power_sem.at[1], partner
+    ).wait_send()
+    remote(out_core, got, core_send, core_recv.at[0, 0], partner).wait_send()
     four_copy.wait_send()
     for k in range(STEPS):
         remote(senders[k], receivers[k], step_send.at[k], step_recv.at[k, 0], partner).wait_send()
@@ -486,21 +492,20 @@
         scratch_shapes=[
             pltpu.VMEM((tiles, cycles, orders, LANES), BF16),
             pltpu.VMEM((maps, cycles, coarse, width), F32),
-            pltpu.VMEM(first.shape, F32),
+            pltpu.VMEM(first.shape, BF16),
             pltpu.VMEM(high.shape, BF16),
             pltpu.VMEM(low.shape, BF16),
-            pltpu.VMEM((BLOCKS, 8, 256), F32),
-            pltpu.VMEM((BLOCKS, 128, orders), BF16),
-            pltpu.VMEM((BLOCKS, cycles, 128, LANES), BF16),
-            pltpu.VMEM((BLOCKS, cycles, 128, LANES), BF16),
-            pltpu.VMEM((BLOCKS, cycles, 128, LANES), BF16),
+            pltpu.VMEM((2 * tiles, 8, 256), F32),
+            pltpu.VMEM((2, tiles, 256, orders), BF16),
+            pltpu.VMEM((2, tiles, HALVES, cycles, 64, LANES), BF16),
+            pltpu.VMEM((2, tiles, HALVES, cycles, 64, LANES), BF16),
+            pltpu.VMEM((2, tiles, HALVES, cycles, 64, LANES), BF16),
             pltpu.VMEM((cycles * channels, orders), BF16),
             pltpu.VMEM((cycles * channels, orders), BF16),
-            pltpu.VMEM((BLOCKS, 2 * cycles * channels, 128), F32),
             *steps((512, 256, 128, 64)),
             pltpu.VMEM((BLOCKS, 3, 16, LANES), BF16),
             pltpu.VMEM((BLOCKS, 3, 16, LANES), BF16),
-            pltpu.VMEM((BLOCKS, 256, LANES), F32),
+            pltpu.VMEM((BLOCKS, 512, LANES), F32),
             pltpu.VMEM((ells // 128, 16, 128), F32),
             pltpu.VMEM((ells // 128, 16, 128), F32),
             pltpu.VMEM((16, 128), F32),
@@ -508,7 +513,7 @@
             pltpu.SemaphoreType.DMA((tiles,)),
             pltpu.SemaphoreType.DMA((4,)),
             pltpu.SemaphoreType.DMA,
-            pltpu.SemaphoreType.DMA((BLOCKS,)),
+            pltpu.SemaphoreType.DMA((2, tiles)),
             pltpu.SemaphoreType.DMA((2,)),
             pltpu.SemaphoreType.DMA((STEPS,)),
             pltpu.SemaphoreType.DMA((STEPS, BLOCKS)),

time: 70.4 us -> 66.8 us (0.949)
  Pallas kernels: 66.5 us -> 63 us
    pallas_call x1, Pallas kernels: 66.5 us -> 63 us  [main_call(): pl.pallas_call(functools.partial(main_body, maps, cycles, orders), out_sh...]
where the time goes in v2:
time: 66.8 us; the launch traced here: 66.6 us
  Pallas kernels  63 us (94%)
  local copies, waits for them, and re-layouts  2.97 us (4%)
    pallas_call x1, Pallas kernels, main_call(): pl.pallas_call(functools.partial(main_body, maps, cycles, orders), out_sh...  63 us
    unnamed x2, local copies, waits for them, and re-layouts  2.97 us

profile of v2, /device:TPU:7, one launch (start us, length us, event | category | flops | bytes accessed | tf_op | source)
XLA Modules:
  0.0 66.6 jit_solution(18171906508991007638)
XLA Ops:
  0.6 63.0 %shard_map.86 = (f32[4,4,2,2048]{3,2,1,0:T(2,128)}, f32[10,16]{1,0:T(8,128)}) custom-call(bf16[4,512,2048]{2,1,0:T(8,128)(2,1)} %legendre_ref.1, f32[4,4,4096]{2,1,0:T(4,128)} %sky_ref.1, bf16[2,64,32]{2,1,0:T(8,128)(2,1)} %constant.8.clone.first_ref, bf16[256,1024]{1,0:T(8,128)(2,1)} %constant.9.clone.high_ref, bf16[256,1024]{1,0:T(8,128)(2,1)} %constant.10.clone.low_ref, ...), custom_call_target="tpu_custom_call" | custom-call | flops 10000000000 | bytes 16777216 | tf_op jit(solution)/shard_map/pallas_call | solution.py:484
  63.6 1.7 %copy.11 = f32[4,4,2,2048]{3,2,1,0:T(2,128)} copy(f32[4,4,2,2048]{3,2,1,0:T(2,128)} %get-tuple-element.4) | data formatting | bytes 524288
  65.3 1.3 %copy.12 = f32[10,16]{1,0:T(8,128)} copy(f32[10,16]{1,0:T(8,128)} %get-tuple-element.5) | data formatting | bytes 1280

commit v3 on v2

--- a/solution.py
+++ b/solution.py
@@ -19,10 +19,24 @@
 BLOCKS = 16
 STEPS = 4
 ORDERS = (
-    (0, 4, 3, 2, 1, 5), (1, 4, 5, 0, 2, 3), (2, 3, 4, 1, 0, 5), (3, 1, 2, 5, 4, 0),
-    (4, 1, 0, 3, 2, 5), (5, 4, 3, 2, 0, 1), (0, 5, 2, 3, 1, 4), (1, 3, 4, 5, 0, 2),
-    (2, 0, 4, 5, 3, 1), (3, 5, 1, 0, 4, 2), (4, 2, 1, 5, 0, 3), (5, 2, 0, 3, 4, 1),
-    (0, 5, 1, 3, 2, 4), (1, 0, 5, 4, 2, 3), (2, 4, 0, 1, 3, 5), (3, 5, 2, 4, 0, 1),
+    (5, 4, 1, 2, 3, 0), (0, 1, 3, 5, 4, 2), (5, 0, 3, 1, 4, 2), (1, 3, 5, 0, 2, 4),
+    (0, 4, 2, 3, 1, 5), (3, 1, 2, 4, 0, 5), (1, 0, 3, 2, 4, 5), (4, 2, 5, 3, 1, 0),
+    (1, 4, 5, 0, 2, 3), (2, 5, 1, 0, 4, 3), (3, 5, 1, 2, 0, 4), (5, 2, 0, 3, 4, 1),
+    (2, 3, 1, 0, 4, 5), (3, 2, 5, 1, 0, 4), (0, 2, 1, 3, 4, 5), (4, 1, 3, 2, 5, 0),
+)
+
+PROGRAM = (
+    ("F", 0, 0), ("F", 1, 0), ("F", 2, 0), ("F", 3, 0), ("F", 4, 0), ("F", 5, 0), ("F", 6, 0), ("F", 7, 0),
+    ("K", 0, 0), ("S", 0, 0), ("S", 1, 0), ("K", 1, 0), ("S", 3, 0), ("K", 2, 0), ("K", 3, 0), ("S", 5, 0),
+    ("S", 2, 0), ("K", 4, 0), ("S", 7, 0), ("K", 5, 0), ("S", 4, 0), ("S", 9, 0), ("K", 6, 0), ("S", 6, 0),
+    ("K", 7, 0), ("S", 10, 0), ("S", 11, 0), ("S", 15, 0), ("S", 12, 0), ("S", 14, 0), ("S", 8, 0), ("S", 9, 1),
+    ("S", 0, 1), ("S", 7, 1), ("S", 2, 1), ("S", 13, 0), ("S", 1, 1), ("S", 10, 1), ("S", 4, 1), ("S", 11, 1),
+    ("S", 6, 1), ("S", 3, 1), ("S", 7, 2), ("S", 5, 1), ("S", 14, 1), ("S", 8, 1), ("S", 12, 1), ("S", 13, 1),
+    ("S", 15, 1), ("S", 11, 2), ("S", 2, 2), ("S", 9, 2), ("S", 4, 2), ("S", 1, 2), ("S", 0, 2), ("S", 3, 2),
+    ("S", 6, 2), ("S", 10, 2), ("S", 5, 2), ("S", 7, 3), ("S", 8, 2), ("S", 14, 2), ("S", 15, 2), ("S", 13, 2),
+    ("S", 12, 2), ("S", 2, 3), ("S", 9, 3), ("S", 11, 3), ("S", 1, 3), ("S", 4, 3), ("S", 0, 3), ("S", 3, 3),
+    ("S", 6, 3), ("S", 10, 3), ("S", 5, 3), ("S", 8, 3), ("S", 14, 3), ("S", 15, 3), ("S", 13, 3), ("S", 12, 3),
+    ("E", 0, 0), ("E", 1, 0), ("E", 3, 0), ("E", 5, 0), ("E", 2, 0), ("E", 4, 0), ("E", 7, 0), ("E", 6, 0),
 )
 
 
@@ -67,36 +81,22 @@
     return ((x * 4 + y) * 2 + z % 2) * 2 + core, z // 2
 
 
-def moved(chip, gen):
-    axis, kind = gen % 3, gen // 3
-    out = []
-    for i, c in enumerate(chip):
-        if isinstance(gen, int):
-            out.append((c + 1 - 2 * (c % 2) if kind == 0 else 3 - c) if axis == i else c)
-            continue
-        other = jnp.where(kind == 0, c + 1 - 2 * (c % 2), 3 - c)
-        out.append(jnp.where(axis == i, other, c))
-    return tuple(out)
-
-
-def look_up(values, index):
-    total = jnp.int32(0)
-    for i, value in enumerate(values):
-        if value:
-            total = total + jnp.where(index == i, jnp.int32(value), jnp.int32(0))
-    return total
+def moved(chip, core, gen):
+    axis, c = gen % 3, chip[gen % 3]
+    other = jnp.where((gen // 3 + core) % 2 == 0, c + 1 - 2 * (c % 2), 3 - c)
+    return chip[:axis] + (other,) + chip[axis + 1 :]
 
 
 def row_flips():
-    out = np.zeros((2, BLOCKS // HALVES, HALVES, 2, 32, 2), np.int32)
-    for half, t, h, part, low, j in np.ndindex(*out.shape):
+    out = np.zeros((2, 2, BLOCKS // HALVES, HALVES, 2, 32, 2), np.int32)
+    for core, half, t, h, part, low, j in np.ndindex(*out.shape):
         flips = [0, 0, 0]
         for k, gen in enumerate(ORDERS[HALVES * t + h]):
             if ((half * 32 + low) >> (5 - k)) & 1:
-                flips[gen % 3] ^= 1 if gen // 3 == 0 else 3
+                flips[gen % 3] ^= 1 if (gen // 3 + core + part) % 2 == 0 else 3
         device = ((flips[0] * 4 + flips[1]) * 2 + flips[2] % 2) * 4 + part * 2 + flips[2] // 2
-        out[half, t, h, part, low, j] = device * 4 + h * 2 + j
-    return out.reshape(-1, 256)
+        out[core, half, t, h, part, low, j] = device * 4 + h * 2 + j
+    return out.reshape(2, -1, 256)
 
 
 def spectral_values(x_ref, first, high, low):
@@ -136,7 +136,11 @@
     first_buf,
     high_buf,
     low_buf,
+    flips,
+    table,
+    harm,
     lines,
+    coefs,
     hot,
     own,
     out_core,
@@ -160,6 +164,7 @@
     column_got,
     leg_sem,
     in_sem,
+    out_sem,
     core_send,
     core_recv,
     four_sem,
@@ -184,8 +189,13 @@
             legendre_ref.at[:, :, pl.ds(pl.multiple_of(t * LANES, LANES), LANES)], leg.at[t], leg_sem.at[t]
         )
 
-    leg_copy(0).start()
     coarse = sky.shape[2]
+    small = [
+        pltpu.make_async_copy(flips_ref.at[core], flips, in_sem.at[1]),
+        pltpu.make_async_copy(table_ref, table, in_sem.at[2]),
+    ]
+    for load in small:
+        load.start()
 
     def sky_copy(k, carry):
         lanes = pl.ds(pl.multiple_of(k * 128, 128), 128)
@@ -193,19 +203,18 @@
         return carry
 
     loads = [
-        pltpu.make_async_copy(src, dst, in_sem.at[i + 1])
+        pltpu.make_async_copy(src, dst, in_sem.at[i + 3])
         for i, (src, dst) in enumerate([(first_ref, first_buf), (high_ref, high_buf), (low_ref, low_buf)])
     ]
     lax.fori_loop(0, coarse, sky_copy, 0)
     for load in loads:
         load.start()
     loads.append(pltpu.make_async_copy(sky, sky, in_sem.at[0]))
-    for t in range(1, tiles):
-        leg_copy(t).start()
+    leg_copy(0).start()
 
     barrier = pltpu.get_barrier_semaphore()
     partner = device_at(x, y, z, 1 - core)
-    across = [device_at(*moved(chip, g), core) for g in range(6)]
+    across = [device_at(*moved(chip, core, g), core) for g in range(6)]
     near = [partner] + across
     for device in near:
         pl.semaphore_signal(barrier, inc=1, device_id=device, device_id_type=MESH)
@@ -218,33 +227,42 @@
     def core_copy(half, t):
         return remote(out_core.at[half, t], got.at[half, t], core_send, core_recv.at[half, t], partner)
 
-    def make_hot(half, t):
-        column = jnp.transpose(lines[half * tiles + t])[:, 0:1].astype(I32)
+    def make_hot(i):
+        column = jnp.transpose(lines[i])[:, 0:1].astype(I32)
         lane = lax.broadcasted_iota(I32, (256, orders), 1)
-        hot[half, t] = jnp.where(column == lane, 1.0, 0.0).astype(BF16)
-
-    def permute(half, t):
-        one_hot = hot[half, t]
+        hot[i % 3] = jnp.where(column == lane, 1.0, 0.0).astype(BF16)
+
+    def permute(i):
+        half, t = 1 - i // tiles, i % tiles
+        if half:
+            leg_copy(t).wait()
+        one_hot = hot[i % 3]
         for r in range(cycles):
             picked = jnp.dot(one_hot, leg[t, r], preferred_element_type=F32).astype(BF16)
             for h in range(HALVES):
                 own[half, t, h, r] = picked[128 * h : 128 * h + 64]
                 out_core[half, t, h, r] = picked[128 * h + 64 : 128 * (h + 1)]
+        core_copy(half, t).start()
 
     base = ((place * 2 + z % 2) * 4 + core * 2 + z // 2) * 4
-    digits = jnp.concatenate([table_ref[...] >> 4, table_ref[...] & 15], axis=0).astype(F32).astype(BF16)
+    for load in small:
+        load.wait()
+    digits = jnp.concatenate([table[...] >> 4, table[...] & 15], axis=0).astype(F32).astype(BF16)
     for i in range(2 * tiles):
-        slot = flips_ref[i : i + 1, :] ^ base
+        row = (1 - i // tiles) * tiles + i % tiles
+        slot = flips[row : row + 1, :] ^ base
         spot = jnp.where(lax.broadcasted_iota(I32, (128, 256), 0) == (slot & 127), 1.0, 0.0).astype(BF16)
         found = jnp.dot(digits, spot, preferred_element_type=F32)
         found = found[0:4] * 16.0 + found[4:8]
         found = jnp.where(lax.broadcasted_iota(I32, (4, 256), 0) == (slot >> 7), found, 0.0)
         lines[i] = jnp.broadcast_to(jnp.sum(found, axis=0, keepdims=True), (8, 256))
-    for t in range(2):
-        make_hot(1, t)
+    for i in range(2):
+        make_hot(i)
 
     for load in loads:
         load.wait()
+    for t in range(1, tiles):
+        leg_copy(t).start()
     spectral = spectral_values(sky, first_buf, high_buf[...], low_buf[...])
     rows = maps * cycles
     out_row = lax.broadcasted_iota(I32, (cycles * channels, rows), 0)
@@ -258,23 +276,21 @@
     pl.semaphore_wait(barrier, len(near))
     four_copy = remote(four, four_got, four_sem.at[0], four_sem.at[1], partner)
     four_copy.start()
-    leg_copy(0).wait()
-    permute(1, 0)
-    core_copy(1, 0).start()
-
-    def coefficients(half, t):
+    permute(0)
+
+    def coefficients(i):
         every = jnp.concatenate([four[...], four_got[...]], axis=0)
-        mine = jnp.concatenate([hot[half, t, 128 * h : 128 * h + 64, :] for h in range(HALVES)], axis=0)
-        return lax.dot_general(every, mine, (((1,), (1,)), ((), ())), preferred_element_type=F32)
-
-    def partial(half, t, coefs, g):
+        mine = jnp.concatenate([hot[i % 3, 128 * h : 128 * h + 64, :] for h in range(HALVES)], axis=0)
+        coefs[i] = lax.dot_general(every, mine, (((1,), (1,)), ((), ())), preferred_element_type=F32)
+
+    def partial(i, g):
         lane = lax.broadcasted_iota(I32, (channels, 128), 1) // 32
         sides = []
         for side in range(2):
             total = jnp.zeros((channels, 128), F32)
             for q in range(4):
                 r = side * 4 + q
-                piece = coefs[r * channels : (r + 1) * channels, :]
+                piece = coefs[i, r * channels : (r + 1) * channels, :]
                 shift = (32 * (q - g)) % 128
                 piece = pltpu.roll(piece, shift, 1) if shift else piece
                 total = jnp.where(lane == q, piece, total)
@@ -286,89 +302,62 @@
         left = jnp.where(row == col, wide, 0.0).astype(BF16)
         at = slice(32 * (g % 2), 32 * (g % 2) + 32)
         right = jnp.concatenate(
-            [ref[half, t, g // 2, r, at, :] for ref in (own, got) for r in range(cycles)], axis=0
+            [ref[1 - i // tiles, i % tiles, g // 2, r, at, :] for ref in (own, got) for r in range(cycles)], axis=0
         )
         return jnp.dot(left, right, preferred_element_type=F32)
 
     senders, receivers = (s1, s2, s3, s4), (r1, r2, r3, r4)
 
     def step_copy(k, b):
-        if isinstance(b, int):
-            device = across[ORDERS[b][k]]
-        else:
-            device = device_at(*moved(chip, look_up([order[k] for order in ORDERS], b)), core)
+        device = across[ORDERS[b][k]]
         return remote(senders[k].at[b], receivers[k].at[b], step_send.at[k], step_recv.at[k, b], device)
 
     four_copy.wait_recv()
-
-    def front(t, carry):
-        @pl.when(t + 1 < tiles)
-        def _():
-            leg_copy(t + 1).wait()
-            permute(1, t + 1)
-            core_copy(1, t + 1).start()
-
-        core_copy(1, t).wait_recv()
-        coefs = coefficients(1, t)
+    coefficients(0)
+
+    def sums(i):
+        half, t = 1 - i // tiles, i % tiles
+        if i + 1 < 2 * tiles:
+            permute(i + 1)
+        core_copy(half, t).wait_recv()
         for g in range(4):
-            s1[HALVES * t + g // 2, (g % 2) * 256 : (g % 2 + 1) * 256] = partial(1, t, coefs, g).astype(BF16)
-        ahead = t + 2
-        make_hot(jnp.where(ahead < tiles, 1, 0), ahead % tiles)
-        for h in range(HALVES):
-            step_copy(0, HALVES * t + h).start()
-        return carry
-
-    lax.fori_loop(0, tiles, front, 0)
-
-    permute(0, 0)
-    core_copy(0, 0).start()
-
-    def second(t, carry):
-        @pl.when(t + 1 < tiles)
-        def _():
-            permute(0, t + 1)
-            core_copy(0, t + 1).start()
-
-        core_copy(0, t).wait_recv()
-        coefs = coefficients(0, t)
-        for g in range(4):
-            acc[HALVES * t + g // 2, (g % 2) * 256 : (g % 2 + 1) * 256] = partial(0, t, coefs, g)
-        make_hot(0, (t + 2) % tiles)
-        for h in range(HALVES):
-            b = HALVES * t + h
-            step_copy(0, b).wait_recv()
-            s2[b] = (acc[b, 256:512] + r1[b, 256:512].astype(F32)).astype(BF16)
-            step_copy(1, b).start()
-            acc[b, 0:256] = acc[b, 0:256] + r1[b, 0:256].astype(F32)
-        return carry
-
-    lax.fori_loop(0, tiles, second, 0)
-
-    for k in (2, 3):
-        n = 512 >> k
-        for b in range(BLOCKS):
-            step_copy(k - 1, b).wait_recv()
-            got_ref = receivers[k - 1]
-            senders[k][b] = (acc[b, n : 2 * n] + got_ref[b, n : 2 * n].astype(F32)).astype(BF16)
-            step_copy(k, b).start()
-            acc[b, 0:n] = acc[b, 0:n] + got_ref[b, 0:n].astype(F32)
+            b, at = HALVES * t + g // 2, slice((g % 2) * 256, (g % 2 + 1) * 256)
+            value = partial(i, g)
+            if half:
+                s1[b, at] = value.astype(BF16)
+            else:
+                acc[b, at] = value
+        if i + 1 < 2 * tiles:
+            coefficients(i + 1)
+        if i + 2 < 2 * tiles:
+            make_hot(i + 2)
+        if half:
+            for h in range(HALVES):
+                step_copy(0, HALVES * t + h).start()
 
     def last_copies(b):
-        near, far = ORDERS[b][5], ORDERS[b][4]
-        to = [across[near], across[far], device_at(*moved(moved(chip, near), far), core)]
+        low, high = ORDERS[b][5], ORDERS[b][4]
+        both = device_at(*moved(moved(chip, core, low), core, high), core)
         return [
             remote(s5.at[b, i], r5.at[b, i], last_send.at[i], last_recv.at[b, i], device)
-            for i, device in enumerate(to)
+            for i, device in enumerate([across[low], across[high], both])
         ]
 
-    for b in range(BLOCKS):
-        step_copy(3, b).wait_recv()
-        total = acc[b, 16:64] + r4[b, 16:64].astype(F32)
-        for i in range(3):
-            s5[b, i] = total[16 * i : 16 * (i + 1)].astype(BF16)
-        for copy in last_copies(b):
-            copy.start()
-        acc[b, 0:16] = acc[b, 0:16] + r4[b, 0:16].astype(F32)
+    def reduce_step(k, b):
+        step_copy(k, b).wait_recv()
+        arrived = receivers[k]
+        if k + 1 < STEPS:
+            n = 256 >> k
+            senders[k + 1][b] = (acc[b, n : 2 * n] + arrived[b, n : 2 * n].astype(F32)).astype(BF16)
+            step_copy(k + 1, b).start()
+        else:
+            n = 16
+            total = acc[b, n : 4 * n] + arrived[b, n : 4 * n].astype(F32)
+            for i in range(3):
+                s5[b, i] = total[n * i : n * (i + 1)].astype(BF16)
+            for copy in last_copies(b):
+                copy.start()
+        acc[b, 0:n] = acc[b, 0:n] + arrived[b, 0:n].astype(F32)
 
     def power_copy(c):
         device = device_at(c // 4, c % 4, z, core)
@@ -396,7 +385,7 @@
             for s in range(2):
                 for a in range(maps):
                     row = s * channels + 2 * a
-                    harm_ref[2 * h + s, a, :, lanes] = value[row : row + 2]
+                    harm[2 * h + s, a, :, lanes] = value[row : row + 2]
             weighted = jnp.where(order == 0, value, 2.0 * value)
             for s in range(2):
                 mode = value[s * channels : (s + 1) * channels]
@@ -420,8 +409,17 @@
             def _():
                 power_copy(c).start()
 
-    for t in range(tiles):
-        finish(t)
+    for kind, which, k in PROGRAM:
+        if kind == "F":
+            sums(which)
+        elif kind == "K":
+            sums(tiles + which)
+        elif kind == "S":
+            reduce_step(k, which)
+        else:
+            finish(which)
+    harm_copy = pltpu.make_async_copy(harm, harm_ref, out_sem.at[0])
+    harm_copy.start()
 
     others = columns - 1
     remote(
@@ -453,6 +451,7 @@
     total = pltpu.roll(total, (128 - share * member) % 128, 1)
     spectra_ref[...] = total[: spectra_ref.shape[0], :share]
 
+    harm_copy.wait()
     whole.wait_send()
     others = columns - 1
     remote(
@@ -487,16 +486,20 @@
             jax.ShapeDtypeStruct((4, maps, 2, ells), F32),
             jax.ShapeDtypeStruct((pairs, ells // devices), F32),
         ],
-        in_specs=[hbm] * 5 + [vmem] * 2 + [pl.BlockSpec(memory_space=pltpu.SMEM)],
-        out_specs=[vmem] * 2,
+        in_specs=[hbm] * 7 + [pl.BlockSpec(memory_space=pltpu.SMEM)],
+        out_specs=[hbm, vmem],
         scratch_shapes=[
             pltpu.VMEM((tiles, cycles, orders, LANES), BF16),
             pltpu.VMEM((maps, cycles, coarse, width), F32),
             pltpu.VMEM(first.shape, BF16),
             pltpu.VMEM(high.shape, BF16),
             pltpu.VMEM(low.shape, BF16),
+            pltpu.VMEM((2 * tiles, 256), I32),
+            pltpu.VMEM((4, 128), I32),
+            pltpu.VMEM((4, maps, 2, ells), F32),
             pltpu.VMEM((2 * tiles, 8, 256), F32),
-            pltpu.VMEM((2, tiles, 256, orders), BF16),
+            pltpu.VMEM((2 * tiles, 2 * cycles * channels, 128), F32),
+            pltpu.VMEM((3, 256, orders), BF16),
             pltpu.VMEM((2, tiles, HALVES, cycles, 64, LANES), BF16),
             pltpu.VMEM((2, tiles, HALVES, cycles, 64, LANES), BF16),
             pltpu.VMEM((2, tiles, HALVES, cycles, 64, LANES), BF16),
@@ -511,7 +514,8 @@
             pltpu.VMEM((16, 128), F32),
             pltpu.VMEM((8, 16, 128), F32),
             pltpu.SemaphoreType.DMA((tiles,)),
-            pltpu.SemaphoreType.DMA((4,)),
+            pltpu.SemaphoreType.DMA((6,)),
+            pltpu.SemaphoreType.DMA((1,)),
             pltpu.SemaphoreType.DMA,
             pltpu.SemaphoreType.DMA((2, tiles)),
             pltpu.SemaphoreType.DMA((2,)),

time: 66.8 us -> 62.6 us (0.937)
  Pallas kernels: 63 us -> 58.7 us
    pallas_call x1, Pallas kernels: 63 us -> 58.7 us  [main_call(): pl.pallas_call(functools.partial(main_body, maps, cycles, orders), out_sh...]
where the time goes in v3:
time: 62.6 us; the launch traced here: 62.4 us
  Pallas kernels  58.7 us (94%)
  local copies, waits for them, and re-layouts  2.97 us (5%)
  between operations  0.64 us (1%)
    pallas_call x1, Pallas kernels, main_call(): pl.pallas_call(functools.partial(main_body, maps, cycles, orders), out_sh...  58.7 us
    unnamed x2, local copies, waits for them, and re-layouts  2.97 us

profile of v3, /device:TPU:7, one launch (start us, length us, event | category | flops | bytes accessed | tf_op | source)
XLA Modules:
  0.0 62.4 jit_solution(11969606095461656240)
XLA Ops:
  0.6 58.7 %shard_map.86 = (f32[4,4,2,2048]{3,2,1,0:T(2,128)}, f32[10,16]{1,0:T(8,128)}) custom-call(bf16[4,512,2048]{2,1,0:T(8,128)(2,1)} %legendre_ref.1, f32[4,4,4096]{2,1,0:T(4,128)} %sky_ref.1, bf16[2,64,32]{2,1,0:T(8,128)(2,1)} %constant.8.clone.first_ref, bf16[256,1024]{1,0:T(8,128)(2,1)} %constant.9.clone.high_ref, bf16[256,1024]{1,0:T(8,128)(2,1)} %constant.10.clone.low_ref, ...), custom_call_target="tpu_custom_call" | custom-call | flops 10000000000 | bytes 16777216 | tf_op jit(solution)/shard_map/pallas_call | solution.py:483
  59.4 1.7 %copy.11 = f32[4,4,2,2048]{3,2,1,0:T(2,128)} copy(f32[4,4,2,2048]{3,2,1,0:T(2,128)} %get-tuple-element.4) | data formatting | bytes 524288
  61.1 1.3 %copy.12 = f32[10,16]{1,0:T(8,128)} copy(f32[10,16]{1,0:T(8,128)} %get-tuple-element.5) | data formatting | bytes 1280

commit v4 on v3

--- a/solution.py
+++ b/solution.py
@@ -52,7 +52,7 @@
     return dot(high, right_high) + (dot(high, right_low) + dot(low, right_high))
 
 
-def fourier_tables(pixels, order_count, width):
+def tables(pixels, order_count, width):
     coarse = pixels // width
     k1, m1 = np.meshgrid(np.arange(coarse), np.arange(coarse), indexing="ij")
     angle = 2.0 * math.pi * ((k1 * m1) % coarse) / coarse
@@ -61,13 +61,14 @@
     m = np.arange(order_count)[None, :]
     angle = 2.0 * math.pi * ((k2 * m) % pixels) / pixels
     cosine, sine = np.cos(angle) / math.sqrt(pixels), np.sin(angle) / math.sqrt(pixels)
-    second = np.block([[cosine, -sine], [sine, cosine]]).astype(np.float32)
-    high = second.astype(BF16)
-    low = (second - high.astype(np.float32)).astype(BF16)
-    first = first.astype(np.float32)
-    first_high = first.astype(BF16)
-    first_low = (first - first_high.astype(np.float32)).astype(BF16)
-    return np.stack([first_high, first_low]), high, low
+    second = np.block([[cosine, -sine], [sine, cosine]])
+    out = np.zeros((second.shape[0] + first.shape[0], second.shape[1]), np.float32)
+    out[: second.shape[0]] = second
+    out[second.shape[0] :, :coarse] = first
+    flips = row_flips()
+    for core in range(2):
+        out[second.shape[0] : second.shape[0] + flips.shape[1], 256 * (core + 1) : 256 * (core + 2)] = flips[core]
+    return out
 
 
 def position():
@@ -99,18 +100,17 @@
     return out.reshape(2, -1, 256)
 
 
-def spectral_values(x_ref, first, high, low):
+def spectral_values(x_ref, first, second):
     maps, cycles, coarse, width = x_ref.shape
     rows = maps * cycles
-    columns = high.shape[1]
-    x_high, x_low = split_bf16(jnp.concatenate([x_ref[i // cycles, i % cycles] for i in range(rows)], axis=1))
-    dot = functools.partial(jnp.dot, preferred_element_type=F32)
-    stage = dot(first[0], x_high) + (dot(first[0], x_low) + dot(first[1], x_high))
+    columns = second.shape[1]
+    spread = jnp.concatenate([x_ref[i // cycles, i % cycles] for i in range(rows)], axis=1)
+    stage = dot3(first[:, :coarse], *split_bf16(spread))
     stages = []
     for i in range(rows):
         piece = stage[:, i * width : (i + 1) * width]
         stages.append(jnp.concatenate([piece[:coarse], piece[coarse:]], axis=1))
-    full = dot3(jnp.concatenate(stages, axis=0), high, low)
+    full = dot3(jnp.concatenate(stages, axis=0), *split_bf16(second))
     m1 = lax.broadcasted_iota(I32, (1, coarse, columns), 1)
     col = lax.broadcasted_iota(I32, (1, coarse, columns), 2)
     full = jnp.where((col % coarse) == m1, full.reshape(rows, coarse, columns), 0.0)
@@ -123,22 +123,18 @@
     orders,
     legendre_ref,
     sky_ref,
-    first_ref,
-    high_ref,
-    low_ref,
-    flips_ref,
+    tables_ref,
     table_ref,
     owner_ref,
     harm_ref,
     spectra_ref,
     leg,
     sky,
+    second_buf,
     first_buf,
-    high_buf,
-    low_buf,
     flips,
     table,
-    harm,
+    owner,
     lines,
     coefs,
     hot,
@@ -164,7 +160,6 @@
     column_got,
     leg_sem,
     in_sem,
-    out_sem,
     core_send,
     core_recv,
     four_sem,
@@ -190,27 +185,30 @@
         )
 
     coarse = sky.shape[2]
+    depth = second_buf.shape[0]
+    mine = pl.ds(pl.multiple_of(256 * (core + 1), 256), 256)
     small = [
-        pltpu.make_async_copy(flips_ref.at[core], flips, in_sem.at[1]),
+        pltpu.make_async_copy(tables_ref.at[pl.ds(depth, 2 * tiles), mine], flips, in_sem.at[1]),
         pltpu.make_async_copy(table_ref, table, in_sem.at[2]),
+    ]
+    loads = [
+        pltpu.make_async_copy(tables_ref.at[pl.ds(0, depth)], second_buf, in_sem.at[3]),
+        pltpu.make_async_copy(tables_ref.at[pl.ds(depth, first_buf.shape[0]), pl.ds(0, 128)], first_buf, in_sem.at[4]),
+        pltpu.make_async_copy(owner_ref, owner, in_sem.at[5]),
     ]
     for load in small:
         load.start()
+    leg_copy(0).start()
 
     def sky_copy(k, carry):
         lanes = pl.ds(pl.multiple_of(k * 128, 128), 128)
         pltpu.make_async_copy(sky_ref.at[:, :, lanes], sky.at[:, :, k, :], in_sem.at[0]).start()
         return carry
 
-    loads = [
-        pltpu.make_async_copy(src, dst, in_sem.at[i + 3])
-        for i, (src, dst) in enumerate([(first_ref, first_buf), (high_ref, high_buf), (low_ref, low_buf)])
-    ]
     lax.fori_loop(0, coarse, sky_copy, 0)
     for load in loads:
         load.start()
     loads.append(pltpu.make_async_copy(sky, sky, in_sem.at[0]))
-    leg_copy(0).start()
 
     barrier = pltpu.get_barrier_semaphore()
     partner = device_at(x, y, z, 1 - core)
@@ -250,7 +248,7 @@
     digits = jnp.concatenate([table[...] >> 4, table[...] & 15], axis=0).astype(F32).astype(BF16)
     for i in range(2 * tiles):
         row = (1 - i // tiles) * tiles + i % tiles
-        slot = flips[row : row + 1, :] ^ base
+        slot = flips[row : row + 1, :].astype(I32) ^ base
         spot = jnp.where(lax.broadcasted_iota(I32, (128, 256), 0) == (slot & 127), 1.0, 0.0).astype(BF16)
         found = jnp.dot(digits, spot, preferred_element_type=F32)
         found = found[0:4] * 16.0 + found[4:8]
@@ -259,11 +257,13 @@
     for i in range(2):
         make_hot(i)
 
+    pl.semaphore_wait(barrier, len(near))
+    permute(0)
     for load in loads:
         load.wait()
     for t in range(1, tiles):
         leg_copy(t).start()
-    spectral = spectral_values(sky, first_buf, high_buf[...], low_buf[...])
+    spectral = spectral_values(sky, first_buf[...], second_buf[...])
     rows = maps * cycles
     out_row = lax.broadcasted_iota(I32, (cycles * channels, rows), 0)
     in_row = lax.broadcasted_iota(I32, (cycles * channels, rows), 1)
@@ -273,10 +273,8 @@
         pick = jnp.where(out_row == wanted, 1.0, 0.0).astype(BF16)
         value = value + jnp.dot(pick, spectral[:, q * orders : (q + 1) * orders], preferred_element_type=F32)
     four[...] = value.astype(BF16)
-    pl.semaphore_wait(barrier, len(near))
     four_copy = remote(four, four_got, four_sem.at[0], four_sem.at[1], partner)
     four_copy.start()
-    permute(0)
 
     def coefficients(i):
         every = jnp.concatenate([four[...], four_got[...]], axis=0)
@@ -312,13 +310,13 @@
         device = across[ORDERS[b][k]]
         return remote(senders[k].at[b], receivers[k].at[b], step_send.at[k], step_recv.at[k, b], device)
 
-    four_copy.wait_recv()
-    coefficients(0)
-
     def sums(i):
         half, t = 1 - i // tiles, i % tiles
         if i + 1 < 2 * tiles:
             permute(i + 1)
+        if i == 0:
+            four_copy.wait_recv()
+            coefficients(0)
         core_copy(half, t).wait_recv()
         for g in range(4):
             b, at = HALVES * t + g // 2, slice((g % 2) * 256, (g % 2 + 1) * 256)
@@ -379,13 +377,13 @@
             value = acc[b, 0:16]
             for i in range(3):
                 value = value + r5[b, i].astype(F32)
-            pair = [owner_ref[base + 2 * h + s] for s in range(2)]
+            pair = [owner[base + 2 * h + s] for s in range(2)]
             order = jnp.where(lax.broadcasted_iota(I32, (2 * channels, 1), 0) < channels, pair[0], pair[1])
             value = jnp.where(ell >= order, value, 0.0)
             for s in range(2):
                 for a in range(maps):
                     row = s * channels + 2 * a
-                    harm[2 * h + s, a, :, lanes] = value[row : row + 2]
+                    harm_ref[2 * h + s, a, :, lanes] = value[row : row + 2]
             weighted = jnp.where(order == 0, value, 2.0 * value)
             for s in range(2):
                 mode = value[s * channels : (s + 1) * channels]
@@ -418,8 +416,6 @@
             reduce_step(k, which)
         else:
             finish(which)
-    harm_copy = pltpu.make_async_copy(harm, harm_ref, out_sem.at[0])
-    harm_copy.start()
 
     others = columns - 1
     remote(
@@ -451,7 +447,6 @@
     total = pltpu.roll(total, (128 - share * member) % 128, 1)
     spectra_ref[...] = total[: spectra_ref.shape[0], :share]
 
-    harm_copy.wait()
     whole.wait_send()
     others = columns - 1
     remote(
@@ -473,8 +468,8 @@
     channels = 2 * maps
     tiles = ells // LANES
     pairs = maps * (maps + 1) // 2
-    first, high, low = fourier_tables(pixels, orders, width)
-    hbm = pl.BlockSpec(memory_space=pl.ANY)
+    constants = tables(pixels, orders, width)
+    hbm = pl.BlockSpec(memory_space=pltpu.HBM)
     vmem = pl.BlockSpec(memory_space=pltpu.VMEM)
 
     def steps(rows_of):
@@ -486,17 +481,16 @@
             jax.ShapeDtypeStruct((4, maps, 2, ells), F32),
             jax.ShapeDtypeStruct((pairs, ells // devices), F32),
         ],
-        in_specs=[hbm] * 7 + [pl.BlockSpec(memory_space=pltpu.SMEM)],
-        out_specs=[hbm, vmem],
+        in_specs=[hbm] * 5,
+        out_specs=[vmem] * 2,
         scratch_shapes=[
             pltpu.VMEM((tiles, cycles, orders, LANES), BF16),
             pltpu.VMEM((maps, cycles, coarse, width), F32),
-            pltpu.VMEM(first.shape, BF16),
-            pltpu.VMEM(high.shape, BF16),
-            pltpu.VMEM(low.shape, BF16),
-            pltpu.VMEM((2 * tiles, 256), I32),
+            pltpu.VMEM((2 * width, 2 * orders), F32),
+            pltpu.VMEM((2 * coarse, 128), F32),
+            pltpu.VMEM((2 * tiles, 256), F32),
             pltpu.VMEM((4, 128), I32),
-            pltpu.VMEM((4, maps, 2, ells), F32),
+            pltpu.SMEM((orders,), I32),
             pltpu.VMEM((2 * tiles, 8, 256), F32),
             pltpu.VMEM((2 * tiles, 2 * cycles * channels, 128), F32),
             pltpu.VMEM((3, 256, orders), BF16),
@@ -515,7 +509,6 @@
             pltpu.VMEM((8, 16, 128), F32),
             pltpu.SemaphoreType.DMA((tiles,)),
             pltpu.SemaphoreType.DMA((6,)),
-            pltpu.SemaphoreType.DMA((1,)),
             pltpu.SemaphoreType.DMA,
             pltpu.SemaphoreType.DMA((2, tiles)),
             pltpu.SemaphoreType.DMA((2,)),
@@ -527,16 +520,13 @@
             pltpu.SemaphoreType.DMA((2,)),
         ],
         compiler_params=pltpu.CompilerParams(
-            collective_id=0, has_side_effects=True, vmem_limit_bytes=58 * MIB
+            collective_id=0, has_side_effects=True, vmem_limit_bytes=int(53.55 * MIB)
         ),
         cost_estimate=pl.CostEstimate(flops=10_000_000_000, bytes_accessed=16 * MIB, transcendentals=0),
     )(
         legendre,
         sky_maps,
-        jnp.asarray(first),
-        jnp.asarray(high),
-        jnp.asarray(low),
-        jnp.asarray(row_flips()),
+        jnp.asarray(constants),
         owner_table.reshape(4, 128),
         owner_table,
     )

time: 62.6 us -> 60.7 us (0.970)
  local copies, waits for them, and re-layouts: 2.97 us -> 1.98 us
  Pallas kernels: 58.7 us -> 58 us
    unnamed x2 -> x4, local copies, waits for them, and re-layouts: 2.97 us -> 1.98 us
    pallas_call x1, Pallas kernels: 58.7 us -> 58 us  [main_call(): pl.pallas_call(functools.partial(main_body, maps, cycles, orders), out_sh...]
where the time goes in v4:
time: 60.7 us; the launch traced here: 60.6 us
  Pallas kernels  58 us (96%)
  local copies, waits for them, and re-layouts  1.98 us (3%)
  between operations  0.65 us (1%)
    pallas_call x1, Pallas kernels, main_call(): pl.pallas_call(functools.partial(main_body, maps, cycles, orders), out_sh...  58 us
    unnamed x4, local copies, waits for them, and re-layouts  1.98 us

profile of v4, /device:TPU:7, one launch (start us, length us, event | category | flops | bytes accessed | tf_op | source)
XLA Modules:
  0.0 60.6 jit_solution(12629744048994770247)
XLA Ops:
  0.6 0.0 copy-start
  0.6 0.7 %copy-done = s32[512]{0:T(512)S(1)} copy-done((s32[512]{0:T(512)S(1)}, s32[512]{0:T(512)}, u32[]{:S(2)}) %copy-start) | copy-done | bytes 2072
  1.3 58.0 %shard_map.59 = (f32[4,4,2,2048]{3,2,1,0:T(2,128)S(1)}, f32[10,16]{1,0:T(8,128)S(1)}) custom-call(bf16[4,512,2048]{2,1,0:T(8,128)(2,1)} %legendre_ref.1, f32[4,4,4096]{2,1,0:T(4,128)} %sky_ref.1, f32[320,1024]{1,0:T(8,128)} %constant.2.clone.tables_ref, s32[4,128]{1,0:T(4,128)S(1)} %bitcast.1, s32[512]{0:T(512)S(1)} %copy-done), custom_call_target="tpu_custom_call" | custom-call | flops 10000000000 | bytes 16777216 | tf_op jit(solution)/shard_map/pallas_call | solution.py:478
  59.3 0.7 %copy.8 = f32[4,4,2,2048]{3,2,1,0:T(2,128)} copy(f32[4,4,2,2048]{3,2,1,0:T(2,128)S(1)} %get-tuple-element.4) | data formatting | bytes 524288
  60.0 0.6 copy.9
Async XLA Ops:
  0.6 0.7 %copy-start = (s32[512]{0:T(512)S(1)}, s32[512]{0:T(512)}, u32[]{:S(2)}) copy-start(s32[512]{0:T(512)} %owner_ref.1) | copy-start | bytes 6148

commit v5 on v4

--- a/solution.py
+++ b/solution.py
@@ -156,8 +156,6 @@
     acc,
     power,
     power_got,
-    column,
-    column_got,
     leg_sem,
     in_sem,
     core_send,
@@ -168,14 +166,13 @@
     last_send,
     last_recv,
     power_sem,
-    column_sem,
 ):
     x, y, z, core = position()
     chip = (x, y, z)
     place = x * 4 + y
     member = ((z % 2) * 2 + core) * 2 + z // 2
-    members = 8
-    columns = power.shape[0]
+    members = power.shape[1]
+    me = place * members + member
     channels = 2 * maps
     tiles = legendre_ref.shape[2] // LANES
 
@@ -337,7 +334,7 @@
         low, high = ORDERS[b][5], ORDERS[b][4]
         both = device_at(*moved(moved(chip, core, low), core, high), core)
         return [
-            remote(s5.at[b, i], r5.at[b, i], last_send.at[i], last_recv.at[b, i], device)
+            remote(s5.at[b, i], r5.at[b, i], last_send.at[i], last_recv.at[b], device)
             for i, device in enumerate([across[low], across[high], both])
         ]
 
@@ -357,14 +354,14 @@
                 copy.start()
         acc[b, 0:n] = acc[b, 0:n] + arrived[b, 0:n].astype(F32)
 
-    def power_copy(c):
-        device = device_at(c // 4, c % 4, z, core)
-        return remote(power.at[c], power_got.at[place], power_sem.at[0], power_sem.at[1], device)
-
-    def column_copy(n):
-        there = (n % 2) * 2 + n // 4
-        device = device_at(x, y, there, (n // 2) % 2)
-        return remote(column, column_got.at[member], column_sem.at[0], column_sem.at[1], device)
+    def power_copy(c, m):
+        there = device_at(c // 4, c % 4, (m % 2) * 2 + m // 4, (m // 2) % 2)
+        self = me == c * members + m
+        device = tuple(jnp.where(self, other, value) for value, other in zip(there, partner))
+        row = jnp.where(self, power_got.shape[0] - 1, me)
+        return remote(power.at[c, m], power_got.at[row], power_sem.at[0], power_sem.at[1], device)
+
+    share = spectra_ref.shape[1]
 
     def finish(t):
         lanes = slice(t * LANES, (t + 1) * LANES)
@@ -372,8 +369,7 @@
         total = [None] * maps
         for h in range(HALVES):
             b = HALVES * t + h
-            for copy in last_copies(b):
-                copy.wait_recv()
+            remote(s5.at[b], r5.at[b], last_send.at[0], last_recv.at[b], partner).wait_recv()
             value = acc[b, 0:16]
             for i in range(3):
                 value = value + r5[b, i].astype(F32)
@@ -397,15 +393,22 @@
             for j in range(i, maps):
                 k, a = (j - i, i) if j - i <= maps // 2 else (maps - (j - i), j)
                 rows.append(total[k][2 * a : 2 * a + 1] + total[k][2 * a + 1 : 2 * a + 2])
-        rows.append(jnp.zeros((power.shape[1] - len(rows), LANES), F32))
-        block = jnp.concatenate(rows, axis=0)
+        group = lax.broadcasted_iota(I32, (members, 128), 1) // share
+        own_group = group == lax.broadcasted_iota(I32, (members, 128), 0)
         for half in range(LANES // 128):
             c = (LANES // 128) * t + half
-            power[c] = block[:, 128 * half : 128 * (half + 1)]
-
-            @pl.when(c != place)
-            def _():
-                power_copy(c).start()
+            sides = [None] * (LANES // 128)
+            for p, row in enumerate(rows):
+                piece = jnp.where(own_group, row[:, 128 * half : 128 * (half + 1)], 0.0)
+                shift = (share * p) % 128
+                piece = pltpu.roll(piece, shift, 1) if shift else piece
+                side = share * p // 128
+                sides[side] = piece if sides[side] is None else sides[side] + piece
+            block = jnp.concatenate(sides, axis=1)
+            for m in range(members):
+                power[c, m] = block[m : m + 1]
+            for m in range(members):
+                power_copy(c, m).start()
 
     for kind, which, k in PROGRAM:
         if kind == "F":
@@ -417,47 +420,26 @@
         else:
             finish(which)
 
-    others = columns - 1
-    remote(
-        power.at[0:others], power_got.at[0:others], power_sem.at[0], power_sem.at[1], partner
-    ).wait_recv()
-    power_got[place] = power[place]
-    total = power_got[0]
-    for c in range(1, columns):
-        total = total + power_got[c]
-    column[...] = total
-    for n in range(members):
-
-        @pl.when(n != member)
-        def _():
-            column_copy(n).start()
-
-    others = members - 1
-    whole = remote(
-        column_got.at[0:others], column_got.at[0:others], column_sem.at[0], column_sem.at[1], partner
-    )
+    others = power_got.shape[0] - 1
+    whole = remote(power_got.at[0:others], power_got.at[0:others], power_sem.at[0], power_sem.at[1], partner)
     whole.wait_recv()
-    column_got[member] = column[...]
-    total = column_got[0]
-    for n in range(1, members):
-        total = total + column_got[n]
-    share = spectra_ref.shape[1]
-    ell = place * 128 + lax.broadcasted_iota(I32, total.shape, 1)
-    total = total / (2 * ell + 1).astype(F32)
-    total = pltpu.roll(total, (128 - share * member) % 128, 1)
-    spectra_ref[...] = total[: spectra_ref.shape[0], :share]
+    power_got[me] = power[place, member]
+    total = jnp.sum(power_got[0:others], axis=0)
+    ell = share * me + lax.broadcasted_iota(I32, (1, 128), 1) % share
+    for side in range(total.shape[1] // 128):
+        line = total[:, 128 * side : 128 * (side + 1)] / (2 * ell + 1).astype(F32)
+        line = pltpu.roll(line, (128 - share * member) % 128, 1)
+        for p in range(128 // share * side, min(128 // share * (side + 1), spectra_ref.shape[0])):
+            shift = (128 - share * p) % 128
+            spectra_ref[p : p + 1, :] = (pltpu.roll(line, shift, 1) if shift else line)[:, :share]
 
     whole.wait_send()
-    others = columns - 1
-    remote(
-        power.at[0:others], power_got.at[0:others], power_sem.at[0], power_sem.at[1], partner
-    ).wait_send()
     remote(out_core, got, core_send, core_recv.at[0, 0], partner).wait_send()
     four_copy.wait_send()
     for k in range(STEPS):
         remote(senders[k], receivers[k], step_send.at[k], step_recv.at[k, 0], partner).wait_send()
     for i in range(3):
-        remote(s5.at[:, i], r5.at[:, i], last_send.at[i], last_recv.at[0, i], partner).wait_send()
+        remote(s5.at[:, i], r5.at[:, i], last_send.at[i], last_recv.at[0], partner).wait_send()
 
 
 def main_call(devices, sky_maps, legendre, owner_table):
@@ -503,10 +485,8 @@
             pltpu.VMEM((BLOCKS, 3, 16, LANES), BF16),
             pltpu.VMEM((BLOCKS, 3, 16, LANES), BF16),
             pltpu.VMEM((BLOCKS, 512, LANES), F32),
-            pltpu.VMEM((ells // 128, 16, 128), F32),
-            pltpu.VMEM((ells // 128, 16, 128), F32),
-            pltpu.VMEM((16, 128), F32),
-            pltpu.VMEM((8, 16, 128), F32),
+            pltpu.VMEM((ells // 128, devices * 128 // ells, 1, LANES), F32),
+            pltpu.VMEM((devices + 1, 1, LANES), F32),
             pltpu.SemaphoreType.DMA((tiles,)),
             pltpu.SemaphoreType.DMA((6,)),
             pltpu.SemaphoreType.DMA,
@@ -515,8 +495,7 @@
             pltpu.SemaphoreType.DMA((STEPS,)),
             pltpu.SemaphoreType.DMA((STEPS, BLOCKS)),
             pltpu.SemaphoreType.DMA((3,)),
-            pltpu.SemaphoreType.DMA((BLOCKS, 3)),
-            pltpu.SemaphoreType.DMA((2,)),
+            pltpu.SemaphoreType.DMA((BLOCKS,)),
             pltpu.SemaphoreType.DMA((2,)),
         ],
         compiler_params=pltpu.CompilerParams(

time: 60.7 us -> 58.5 us (0.964)
  Pallas kernels: 58 us -> 55.7 us
    pallas_call x1, Pallas kernels: 58 us -> 55.7 us  [main_call(): pl.pallas_call(functools.partial(main_body, maps, cycles, orders), out_sh...]
where the time goes in v5:
time: 58.5 us; the launch traced here: 58.4 us
  Pallas kernels  55.7 us (95%)
  local copies, waits for them, and re-layouts  1.98 us (3%)
  between operations  0.65 us (1%)
    pallas_call x1, Pallas kernels, main_call(): pl.pallas_call(functools.partial(main_body, maps, cycles, orders), out_sh...  55.7 us
    unnamed x4, local copies, waits for them, and re-layouts  1.98 us

profile of v5, /device:TPU:7, one launch (start us, length us, event | category | flops | bytes accessed | tf_op | source)
XLA Modules:
  0.0 58.4 jit_solution(13242705274852892933)
XLA Ops:
  0.6 0.0 copy-start
  0.6 0.7 %copy-done = s32[512]{0:T(512)S(1)} copy-done((s32[512]{0:T(512)S(1)}, s32[512]{0:T(512)}, u32[]{:S(2)}) %copy-start) | copy-done | bytes 2072
  1.3 55.7 %shard_map.59 = (f32[4,4,2,2048]{3,2,1,0:T(2,128)S(1)}, f32[10,16]{1,0:T(8,128)S(1)}) custom-call(bf16[4,512,2048]{2,1,0:T(8,128)(2,1)} %legendre_ref.1, f32[4,4,4096]{2,1,0:T(4,128)} %sky_ref.1, f32[320,1024]{1,0:T(8,128)} %constant.2.clone.tables_ref, s32[4,128]{1,0:T(4,128)S(1)} %bitcast.1, s32[512]{0:T(512)S(1)} %copy-done), custom_call_target="tpu_custom_call" | custom-call | flops 10000000000 | bytes 16777216 | tf_op jit(solution)/shard_map/pallas_call | solution.py:460
  57.1 0.7 %copy.8 = f32[4,4,2,2048]{3,2,1,0:T(2,128)} copy(f32[4,4,2,2048]{3,2,1,0:T(2,128)S(1)} %get-tuple-element.4) | data formatting | bytes 524288
  57.8 0.6 %copy.9 = f32[10,16]{1,0:T(8,128)} copy(f32[10,16]{1,0:T(8,128)S(1)} %get-tuple-element.5) | data formatting | bytes 1280
Async XLA Ops:
  0.6 0.7 %copy-start = (s32[512]{0:T(512)S(1)}, s32[512]{0:T(512)}, u32[]{:S(2)}) copy-start(s32[512]{0:T(512)} %owner_ref.1) | copy-start | bytes 6148

commit v6 on v5

--- a/solution.py
+++ b/solution.py
@@ -14,29 +14,34 @@
 MIB = 1024 * 1024
 F32, BF16, I32 = jnp.float32, jnp.bfloat16, jnp.int32
 
-LANES = 256
+WIDTHS = (128, 128, 256, 256, 256, 256, 256, 256, 128, 128)
+TILES = tuple((sum(WIDTHS[:t]), width) for t, width in enumerate(WIDTHS))
 HALVES = 2
-BLOCKS = 16
+BLOCKS = HALVES * len(TILES)
 STEPS = 4
 ORDERS = (
-    (5, 4, 1, 2, 3, 0), (0, 1, 3, 5, 4, 2), (5, 0, 3, 1, 4, 2), (1, 3, 5, 0, 2, 4),
-    (0, 4, 2, 3, 1, 5), (3, 1, 2, 4, 0, 5), (1, 0, 3, 2, 4, 5), (4, 2, 5, 3, 1, 0),
-    (1, 4, 5, 0, 2, 3), (2, 5, 1, 0, 4, 3), (3, 5, 1, 2, 0, 4), (5, 2, 0, 3, 4, 1),
-    (2, 3, 1, 0, 4, 5), (3, 2, 5, 1, 0, 4), (0, 2, 1, 3, 4, 5), (4, 1, 3, 2, 5, 0),
+    (1, 2, 5, 3, 4, 0), (3, 5, 1, 0, 2, 4), (2, 1, 5, 3, 4, 0), (3, 5, 2, 4, 0, 1),
+    (5, 4, 2, 1, 3, 0), (4, 3, 5, 2, 0, 1), (0, 3, 2, 1, 5, 4), (0, 2, 1, 4, 5, 3),
+    (4, 1, 3, 5, 2, 0), (3, 5, 4, 0, 2, 1), (2, 1, 0, 5, 4, 3), (4, 3, 0, 5, 2, 1),
+    (5, 1, 3, 2, 0, 4), (2, 3, 4, 0, 1, 5), (3, 2, 4, 0, 1, 5), (1, 0, 4, 3, 2, 5),
+    (3, 2, 4, 5, 0, 1), (1, 5, 3, 2, 0, 4), (5, 1, 2, 0, 3, 4), (1, 3, 2, 4, 5, 0),
 )
 
 PROGRAM = (
     ("F", 0, 0), ("F", 1, 0), ("F", 2, 0), ("F", 3, 0), ("F", 4, 0), ("F", 5, 0), ("F", 6, 0), ("F", 7, 0),
-    ("K", 0, 0), ("S", 0, 0), ("S", 1, 0), ("K", 1, 0), ("S", 3, 0), ("K", 2, 0), ("K", 3, 0), ("S", 5, 0),
-    ("S", 2, 0), ("K", 4, 0), ("S", 7, 0), ("K", 5, 0), ("S", 4, 0), ("S", 9, 0), ("K", 6, 0), ("S", 6, 0),
-    ("K", 7, 0), ("S", 10, 0), ("S", 11, 0), ("S", 15, 0), ("S", 12, 0), ("S", 14, 0), ("S", 8, 0), ("S", 9, 1),
-    ("S", 0, 1), ("S", 7, 1), ("S", 2, 1), ("S", 13, 0), ("S", 1, 1), ("S", 10, 1), ("S", 4, 1), ("S", 11, 1),
-    ("S", 6, 1), ("S", 3, 1), ("S", 7, 2), ("S", 5, 1), ("S", 14, 1), ("S", 8, 1), ("S", 12, 1), ("S", 13, 1),
-    ("S", 15, 1), ("S", 11, 2), ("S", 2, 2), ("S", 9, 2), ("S", 4, 2), ("S", 1, 2), ("S", 0, 2), ("S", 3, 2),
-    ("S", 6, 2), ("S", 10, 2), ("S", 5, 2), ("S", 7, 3), ("S", 8, 2), ("S", 14, 2), ("S", 15, 2), ("S", 13, 2),
-    ("S", 12, 2), ("S", 2, 3), ("S", 9, 3), ("S", 11, 3), ("S", 1, 3), ("S", 4, 3), ("S", 0, 3), ("S", 3, 3),
-    ("S", 6, 3), ("S", 10, 3), ("S", 5, 3), ("S", 8, 3), ("S", 14, 3), ("S", 15, 3), ("S", 13, 3), ("S", 12, 3),
-    ("E", 0, 0), ("E", 1, 0), ("E", 3, 0), ("E", 5, 0), ("E", 2, 0), ("E", 4, 0), ("E", 7, 0), ("E", 6, 0),
+    ("F", 8, 0), ("F", 9, 0), ("K", 0, 0), ("S", 0, 0), ("S", 1, 0), ("K", 1, 0), ("S", 2, 0), ("S", 3, 0),
+    ("K", 2, 0), ("S", 4, 0), ("S", 5, 0), ("K", 3, 0), ("S", 6, 0), ("K", 4, 0), ("S", 8, 0), ("S", 9, 0),
+    ("K", 5, 0), ("S", 10, 0), ("K", 6, 0), ("S", 7, 0), ("S", 12, 0), ("K", 7, 0), ("S", 11, 0), ("S", 14, 0),
+    ("S", 15, 0), ("K", 8, 0), ("S", 13, 0), ("K", 9, 0), ("S", 16, 0), ("S", 17, 0), ("S", 18, 0), ("S", 1, 1),
+    ("S", 4, 1), ("S", 0, 1), ("S", 5, 1), ("S", 3, 1), ("S", 19, 0), ("S", 2, 1), ("S", 8, 1), ("S", 6, 1),
+    ("S", 7, 1), ("S", 15, 1), ("S", 9, 1), ("S", 10, 1), ("S", 11, 1), ("S", 17, 1), ("S", 12, 1), ("S", 0, 2),
+    ("S", 14, 1), ("S", 13, 1), ("S", 18, 1), ("S", 19, 1), ("S", 5, 2), ("S", 16, 1), ("S", 1, 2), ("S", 15, 2),
+    ("S", 2, 2), ("S", 8, 2), ("S", 4, 2), ("S", 10, 2), ("S", 3, 2), ("S", 17, 2), ("S", 7, 2), ("S", 9, 2),
+    ("S", 6, 2), ("S", 14, 2), ("S", 11, 2), ("S", 18, 2), ("S", 12, 2), ("S", 19, 2), ("S", 0, 3), ("S", 13, 2),
+    ("S", 1, 3), ("S", 5, 3), ("S", 16, 2), ("S", 15, 3), ("S", 2, 3), ("S", 8, 3), ("S", 4, 3), ("S", 3, 3),
+    ("S", 10, 3), ("S", 17, 3), ("S", 7, 3), ("S", 9, 3), ("S", 6, 3), ("S", 14, 3), ("S", 18, 3), ("S", 11, 3),
+    ("S", 19, 3), ("S", 12, 3), ("S", 13, 3), ("S", 16, 3), ("E", 0, 0), ("E", 2, 0), ("E", 1, 0), ("E", 4, 0),
+    ("E", 3, 0), ("E", 7, 0), ("E", 9, 0), ("E", 5, 0), ("E", 6, 0), ("E", 8, 0),
 )
 
 
@@ -89,7 +94,7 @@
 
 
 def row_flips():
-    out = np.zeros((2, 2, BLOCKS // HALVES, HALVES, 2, 32, 2), np.int32)
+    out = np.zeros((2, 2, len(TILES), HALVES, 2, 32, 2), np.int32)
     for core, half, t, h, part, low, j in np.ndindex(*out.shape):
         flips = [0, 0, 0]
         for k, gen in enumerate(ORDERS[HALVES * t + h]):
@@ -174,18 +179,17 @@
     members = power.shape[1]
     me = place * members + member
     channels = 2 * maps
-    tiles = legendre_ref.shape[2] // LANES
+    tiles = len(TILES)
 
     def leg_copy(t):
-        return pltpu.make_async_copy(
-            legendre_ref.at[:, :, pl.ds(pl.multiple_of(t * LANES, LANES), LANES)], leg.at[t], leg_sem.at[t]
-        )
+        lanes = pl.ds(*TILES[t])
+        return pltpu.make_async_copy(legendre_ref.at[:, :, lanes], leg.at[:, :, lanes], leg_sem.at[t])
 
     coarse = sky.shape[2]
     depth = second_buf.shape[0]
     mine = pl.ds(pl.multiple_of(256 * (core + 1), 256), 256)
     small = [
-        pltpu.make_async_copy(tables_ref.at[pl.ds(depth, 2 * tiles), mine], flips, in_sem.at[1]),
+        pltpu.make_async_copy(tables_ref.at[pl.ds(depth, flips.shape[0]), mine], flips, in_sem.at[1]),
         pltpu.make_async_copy(table_ref, table, in_sem.at[2]),
     ]
     loads = [
@@ -220,7 +224,9 @@
         )
 
     def core_copy(half, t):
-        return remote(out_core.at[half, t], got.at[half, t], core_send, core_recv.at[half, t], partner)
+        place_in = (half, slice(None), slice(None), slice(None), pl.ds(*TILES[t]))
+        i = (1 - half) * tiles + t
+        return remote(out_core.at[place_in], got.at[place_in], core_send, core_recv.at[i % 4], partner)
 
     def make_hot(i):
         column = jnp.transpose(lines[i])[:, 0:1].astype(I32)
@@ -232,11 +238,17 @@
         if half:
             leg_copy(t).wait()
         one_hot = hot[i % 3]
-        for r in range(cycles):
-            picked = jnp.dot(one_hot, leg[t, r], preferred_element_type=F32).astype(BF16)
+        first, width = TILES[t]
+        lanes = slice(first, first + width)
+        group = 256 // width
+        for r in range(0, cycles, group):
+            rows = jnp.concatenate([leg[r + n, :, lanes] for n in range(group)], axis=1)
+            picked = jnp.dot(one_hot, rows, preferred_element_type=F32).astype(BF16)
             for h in range(HALVES):
-                own[half, t, h, r] = picked[128 * h : 128 * h + 64]
-                out_core[half, t, h, r] = picked[128 * h + 64 : 128 * (h + 1)]
+                for n in range(group):
+                    part = picked[128 * h : 128 * (h + 1), width * n : width * (n + 1)]
+                    own[half, h, r + n, :, lanes] = part[:64]
+                    out_core[half, h, r + n, :, lanes] = part[64:]
         core_copy(half, t).start()
 
     base = ((place * 2 + z % 2) * 4 + core * 2 + z // 2) * 4
@@ -278,6 +290,9 @@
         mine = jnp.concatenate([hot[i % 3, 128 * h : 128 * h + 64, :] for h in range(HALVES)], axis=0)
         coefs[i] = lax.dot_general(every, mine, (((1,), (1,)), ((), ())), preferred_element_type=F32)
 
+    def lanes_of(t):
+        return slice(TILES[t][0], TILES[t][0] + TILES[t][1])
+
     def partial(i, g):
         lane = lax.broadcasted_iota(I32, (channels, 128), 1) // 32
         sides = []
@@ -296,8 +311,9 @@
         col = lax.broadcasted_iota(I32, (256, 256), 1) % 32
         left = jnp.where(row == col, wide, 0.0).astype(BF16)
         at = slice(32 * (g % 2), 32 * (g % 2) + 32)
+        lanes = lanes_of(i % tiles)
         right = jnp.concatenate(
-            [ref[1 - i // tiles, i % tiles, g // 2, r, at, :] for ref in (own, got) for r in range(cycles)], axis=0
+            [ref[1 - i // tiles, g // 2, r, at, lanes] for ref in (own, got) for r in range(cycles)], axis=0
         )
         return jnp.dot(left, right, preferred_element_type=F32)
 
@@ -305,7 +321,8 @@
 
     def step_copy(k, b):
         device = across[ORDERS[b][k]]
-        return remote(senders[k].at[b], receivers[k].at[b], step_send.at[k], step_recv.at[k, b], device)
+        at = (b % HALVES, slice(None), pl.ds(*TILES[b // HALVES]))
+        return remote(senders[k].at[at], receivers[k].at[at], step_send.at[k], step_recv.at[k, b], device)
 
     def sums(i):
         half, t = 1 - i // tiles, i % tiles
@@ -316,12 +333,12 @@
             coefficients(0)
         core_copy(half, t).wait_recv()
         for g in range(4):
-            b, at = HALVES * t + g // 2, slice((g % 2) * 256, (g % 2 + 1) * 256)
+            at = (g // 2, slice((g % 2) * 256, (g % 2 + 1) * 256), lanes_of(t))
             value = partial(i, g)
             if half:
-                s1[b, at] = value.astype(BF16)
+                s1[at] = value.astype(BF16)
             else:
-                acc[b, at] = value
+                acc[at] = value
         if i + 1 < 2 * tiles:
             coefficients(i + 1)
         if i + 2 < 2 * tiles:
@@ -333,26 +350,29 @@
     def last_copies(b):
         low, high = ORDERS[b][5], ORDERS[b][4]
         both = device_at(*moved(moved(chip, core, low), core, high), core)
+        at, rest = (b % HALVES,), (slice(None), pl.ds(*TILES[b // HALVES]))
         return [
-            remote(s5.at[b, i], r5.at[b, i], last_send.at[i], last_recv.at[b], device)
+            remote(s5.at[at + (i,) + rest], r5.at[at + (i,) + rest], last_send.at[i], last_recv.at[b], device)
             for i, device in enumerate([across[low], across[high], both])
         ]
 
     def reduce_step(k, b):
         step_copy(k, b).wait_recv()
         arrived = receivers[k]
+        h, lanes = b % HALVES, lanes_of(b // HALVES)
         if k + 1 < STEPS:
             n = 256 >> k
-            senders[k + 1][b] = (acc[b, n : 2 * n] + arrived[b, n : 2 * n].astype(F32)).astype(BF16)
+            leaving = acc[h, n : 2 * n, lanes] + arrived[h, n : 2 * n, lanes].astype(F32)
+            senders[k + 1][h, :, lanes] = leaving.astype(BF16)
             step_copy(k + 1, b).start()
         else:
             n = 16
-            total = acc[b, n : 4 * n] + arrived[b, n : 4 * n].astype(F32)
+            leaving = acc[h, n : 4 * n, lanes] + arrived[h, n : 4 * n, lanes].astype(F32)
             for i in range(3):
-                s5[b, i] = total[n * i : n * (i + 1)].astype(BF16)
+                s5[h, i, :, lanes] = leaving[n * i : n * (i + 1)].astype(BF16)
             for copy in last_copies(b):
                 copy.start()
-        acc[b, 0:n] = acc[b, 0:n] + arrived[b, 0:n].astype(F32)
+        acc[h, 0:n, lanes] = acc[h, 0:n, lanes] + arrived[h, 0:n, lanes].astype(F32)
 
     def power_copy(c, m):
         there = device_at(c // 4, c % 4, (m % 2) * 2 + m // 4, (m // 2) % 2)
@@ -364,15 +384,17 @@
     share = spectra_ref.shape[1]
 
     def finish(t):
-        lanes = slice(t * LANES, (t + 1) * LANES)
-        ell = t * LANES + lax.broadcasted_iota(I32, (2 * channels, LANES), 1)
+        first, width = TILES[t]
+        lanes = slice(first, first + width)
+        ell = first + lax.broadcasted_iota(I32, (2 * channels, width), 1)
         total = [None] * maps
         for h in range(HALVES):
             b = HALVES * t + h
-            remote(s5.at[b], r5.at[b], last_send.at[0], last_recv.at[b], partner).wait_recv()
-            value = acc[b, 0:16]
+            at = (h, slice(None), slice(None), pl.ds(first, width))
+            remote(s5.at[at], r5.at[at], last_send.at[0], last_recv.at[b], partner).wait_recv()
+            value = acc[h, 0:16, lanes]
             for i in range(3):
-                value = value + r5[b, i].astype(F32)
+                value = value + r5[h, i, :, lanes].astype(F32)
             pair = [owner[base + 2 * h + s] for s in range(2)]
             order = jnp.where(lax.broadcasted_iota(I32, (2 * channels, 1), 0) < channels, pair[0], pair[1])
             value = jnp.where(ell >= order, value, 0.0)
@@ -395,9 +417,9 @@
                 rows.append(total[k][2 * a : 2 * a + 1] + total[k][2 * a + 1 : 2 * a + 2])
         group = lax.broadcasted_iota(I32, (members, 128), 1) // share
         own_group = group == lax.broadcasted_iota(I32, (members, 128), 0)
-        for half in range(LANES // 128):
-            c = (LANES // 128) * t + half
-            sides = [None] * (LANES // 128)
+        for half in range(width // 128):
+            c = first // 128 + half
+            sides = [None] * (power.shape[3] // 128)
             for p, row in enumerate(rows):
                 piece = jnp.where(own_group, row[:, 128 * half : 128 * (half + 1)], 0.0)
                 shift = (share * p) % 128
@@ -434,7 +456,7 @@
             spectra_ref[p : p + 1, :] = (pltpu.roll(line, shift, 1) if shift else line)[:, :share]
 
     whole.wait_send()
-    remote(out_core, got, core_send, core_recv.at[0, 0], partner).wait_send()
+    remote(out_core, got, core_send, core_recv.at[0], partner).wait_send()
     four_copy.wait_send()
     for k in range(STEPS):
         remote(senders[k], receivers[k], step_send.at[k], step_recv.at[k, 0], partner).wait_send()
@@ -448,14 +470,14 @@
     width = 128
     coarse = pixels // width
     channels = 2 * maps
-    tiles = ells // LANES
+    tiles = len(TILES)
     pairs = maps * (maps + 1) // 2
     constants = tables(pixels, orders, width)
     hbm = pl.BlockSpec(memory_space=pltpu.HBM)
     vmem = pl.BlockSpec(memory_space=pltpu.VMEM)
 
     def steps(rows_of):
-        return [pltpu.VMEM((BLOCKS, n, LANES), BF16) for n in rows_of for _ in range(2)]
+        return [pltpu.VMEM((HALVES, n, ells), BF16) for n in rows_of for _ in range(2)]
 
     return pl.pallas_call(
         functools.partial(main_body, maps, cycles, orders),
@@ -466,31 +488,31 @@
         in_specs=[hbm] * 5,
         out_specs=[vmem] * 2,
         scratch_shapes=[
-            pltpu.VMEM((tiles, cycles, orders, LANES), BF16),
+            pltpu.VMEM((cycles, orders, ells), BF16),
             pltpu.VMEM((maps, cycles, coarse, width), F32),
             pltpu.VMEM((2 * width, 2 * orders), F32),
             pltpu.VMEM((2 * coarse, 128), F32),
-            pltpu.VMEM((2 * tiles, 256), F32),
+            pltpu.VMEM((32, 256), F32),
             pltpu.VMEM((4, 128), I32),
             pltpu.SMEM((orders,), I32),
             pltpu.VMEM((2 * tiles, 8, 256), F32),
             pltpu.VMEM((2 * tiles, 2 * cycles * channels, 128), F32),
             pltpu.VMEM((3, 256, orders), BF16),
-            pltpu.VMEM((2, tiles, HALVES, cycles, 64, LANES), BF16),
-            pltpu.VMEM((2, tiles, HALVES, cycles, 64, LANES), BF16),
-            pltpu.VMEM((2, tiles, HALVES, cycles, 64, LANES), BF16),
+            pltpu.VMEM((2, HALVES, cycles, 64, ells), BF16),
+            pltpu.VMEM((2, HALVES, cycles, 64, ells), BF16),
+            pltpu.VMEM((2, HALVES, cycles, 64, ells), BF16),
             pltpu.VMEM((cycles * channels, orders), BF16),
             pltpu.VMEM((cycles * channels, orders), BF16),
             *steps((512, 256, 128, 64)),
-            pltpu.VMEM((BLOCKS, 3, 16, LANES), BF16),
-            pltpu.VMEM((BLOCKS, 3, 16, LANES), BF16),
-            pltpu.VMEM((BLOCKS, 512, LANES), F32),
-            pltpu.VMEM((ells // 128, devices * 128 // ells, 1, LANES), F32),
-            pltpu.VMEM((devices + 1, 1, LANES), F32),
+            pltpu.VMEM((HALVES, 3, 16, ells), BF16),
+            pltpu.VMEM((HALVES, 3, 16, ells), BF16),
+            pltpu.VMEM((HALVES, 512, ells), F32),
+            pltpu.VMEM((ells // 128, devices * 128 // ells, 1, 256), F32),
+            pltpu.VMEM((devices + 1, 1, 256), F32),
             pltpu.SemaphoreType.DMA((tiles,)),
             pltpu.SemaphoreType.DMA((6,)),
             pltpu.SemaphoreType.DMA,
-            pltpu.SemaphoreType.DMA((2, tiles)),
+            pltpu.SemaphoreType.DMA((4,)),
             pltpu.SemaphoreType.DMA((2,)),
             pltpu.SemaphoreType.DMA((STEPS,)),
             pltpu.SemaphoreType.DMA((STEPS, BLOCKS)),

time: 58.5 us -> 56.5 us (0.966)
  Pallas kernels: 55.7 us -> 53.4 us
    pallas_call x1, Pallas kernels: 55.7 us -> 53.4 us  [main_call(): pl.pallas_call(functools.partial(main_body, maps, cycles, orders), out_sh...]
where the time goes in v6:
time: 56.5 us; the launch traced here: 56 us
  Pallas kernels  53.4 us (95%)
  local copies, waits for them, and re-layouts  1.98 us (4%)
  between operations  0.65 us (1%)
    pallas_call x1, Pallas kernels, main_call(): pl.pallas_call(functools.partial(main_body, maps, cycles, orders), out_sh...  53.4 us
    unnamed x4, local copies, waits for them, and re-layouts  1.98 us

profile of v6, /device:TPU:7, one launch (start us, length us, event | category | flops | bytes accessed | tf_op | source)
XLA Modules:
  0.0 56.0 jit_solution(11780505863546012675)
XLA Ops:
  0.6 0.0 copy-start
  0.6 0.7 %copy-done = s32[512]{0:T(512)S(1)} copy-done((s32[512]{0:T(512)S(1)}, s32[512]{0:T(512)}, u32[]{:S(2)}) %copy-start) | copy-done | bytes 2072
  1.3 53.4 %shard_map.59 = (f32[4,4,2,2048]{3,2,1,0:T(2,128)S(1)}, f32[10,16]{1,0:T(8,128)S(1)}) custom-call(bf16[4,512,2048]{2,1,0:T(8,128)(2,1)} %legendre_ref.1, f32[4,4,4096]{2,1,0:T(4,128)} %sky_ref.1, f32[320,1024]{1,0:T(8,128)} %constant.2.clone.tables_ref, s32[4,128]{1,0:T(4,128)S(1)} %bitcast.1, s32[512]{0:T(512)S(1)} %copy-done), custom_call_target="tpu_custom_call" | custom-call | flops 10000000000 | bytes 16777216 | tf_op jit(solution)/shard_map/pallas_call | solution.py:482
  54.7 0.7 %copy.8 = f32[4,4,2,2048]{3,2,1,0:T(2,128)} copy(f32[4,4,2,2048]{3,2,1,0:T(2,128)S(1)} %get-tuple-element.4) | data formatting | bytes 524288
  55.4 0.6 %copy.9 = f32[10,16]{1,0:T(8,128)} copy(f32[10,16]{1,0:T(8,128)S(1)} %get-tuple-element.5) | data formatting | bytes 1280
Async XLA Ops:
  0.6 0.7 %copy-start = (s32[512]{0:T(512)S(1)}, s32[512]{0:T(512)}, u32[]{:S(2)}) copy-start(s32[512]{0:T(512)} %owner_ref.1) | copy-start | bytes 6148

commit v7 on v6

--- a/solution.py
+++ b/solution.py
@@ -43,6 +43,30 @@
     ("S", 19, 3), ("S", 12, 3), ("S", 13, 3), ("S", 16, 3), ("E", 0, 0), ("E", 2, 0), ("E", 1, 0), ("E", 4, 0),
     ("E", 3, 0), ("E", 7, 0), ("E", 9, 0), ("E", 5, 0), ("E", 6, 0), ("E", 8, 0),
 )
+
+
+def arrival_slots():
+    sent, waited = {}, {}
+    for at, (kind, which, k) in enumerate(PROGRAM):
+        if kind == "F":
+            sent.update({(0, HALVES * which + h): at for h in range(HALVES)})
+        elif kind == "S":
+            waited[k, which] = at
+            if k + 1 < STEPS:
+                sent[k + 1, which] = at
+    gen = {(k, b): ORDERS[b][k] for k, b in sent}
+    slots, last = {}, []
+    for later in sorted(sent, key=lambda m: (sent[m], m)):
+        for slot, earlier in enumerate(last):
+            if any(
+                gen[m] == gen[later] and sent[m] >= waited[earlier] and waited[m] <= sent[later] for m in sent
+            ):
+                break
+        else:
+            slot = len(last)
+            last.append(None)
+        slots[later], last[slot] = slot, later
+    return slots, len(last)
 
 
 def split_bf16(values):
@@ -226,7 +250,7 @@
     def core_copy(half, t):
         place_in = (half, slice(None), slice(None), slice(None), pl.ds(*TILES[t]))
         i = (1 - half) * tiles + t
-        return remote(out_core.at[place_in], got.at[place_in], core_send, core_recv.at[i % 4], partner)
+        return remote(out_core.at[place_in], got.at[place_in], core_send, core_recv.at[i % 8], partner)
 
     def make_hot(i):
         column = jnp.transpose(lines[i])[:, 0:1].astype(I32)
@@ -263,7 +287,7 @@
         found = found[0:4] * 16.0 + found[4:8]
         found = jnp.where(lax.broadcasted_iota(I32, (4, 256), 0) == (slot >> 7), found, 0.0)
         lines[i] = jnp.broadcast_to(jnp.sum(found, axis=0, keepdims=True), (8, 256))
-    for i in range(2):
+    for i in range(3):
         make_hot(i)
 
     pl.semaphore_wait(barrier, len(near))
@@ -284,6 +308,7 @@
     four[...] = value.astype(BF16)
     four_copy = remote(four, four_got, four_sem.at[0], four_sem.at[1], partner)
     four_copy.start()
+    permute(1)
 
     def coefficients(i):
         every = jnp.concatenate([four[...], four_got[...]], axis=0)
@@ -319,15 +344,17 @@
 
     senders, receivers = (s1, s2, s3, s4), (r1, r2, r3, r4)
 
+    slots, _ = arrival_slots()
+
     def step_copy(k, b):
         device = across[ORDERS[b][k]]
         at = (b % HALVES, slice(None), pl.ds(*TILES[b // HALVES]))
-        return remote(senders[k].at[at], receivers[k].at[at], step_send.at[k], step_recv.at[k, b], device)
+        return remote(senders[k].at[at], receivers[k].at[at], step_send.at[k], step_recv.at[slots[k, b]], device)
 
     def sums(i):
         half, t = 1 - i // tiles, i % tiles
-        if i + 1 < 2 * tiles:
-            permute(i + 1)
+        if 0 < i < 2 * tiles - 2:
+            permute(i + 2)
         if i == 0:
             four_copy.wait_recv()
             coefficients(0)
@@ -341,11 +368,13 @@
                 acc[at] = value
         if i + 1 < 2 * tiles:
             coefficients(i + 1)
-        if i + 2 < 2 * tiles:
-            make_hot(i + 2)
+        if i + 3 < 2 * tiles:
+            make_hot(i + 3)
         if half:
             for h in range(HALVES):
                 step_copy(0, HALVES * t + h).start()
+        if i == 0:
+            permute(2)
 
     def last_copies(b):
         low, high = ORDERS[b][5], ORDERS[b][4]
@@ -459,7 +488,7 @@
     remote(out_core, got, core_send, core_recv.at[0], partner).wait_send()
     four_copy.wait_send()
     for k in range(STEPS):
-        remote(senders[k], receivers[k], step_send.at[k], step_recv.at[k, 0], partner).wait_send()
+        remote(senders[k], receivers[k], step_send.at[k], step_recv.at[0], partner).wait_send()
     for i in range(3):
         remote(s5.at[:, i], r5.at[:, i], last_send.at[i], last_recv.at[0], partner).wait_send()
 
@@ -512,10 +541,10 @@
             pltpu.SemaphoreType.DMA((tiles,)),
             pltpu.SemaphoreType.DMA((6,)),
             pltpu.SemaphoreType.DMA,
-            pltpu.SemaphoreType.DMA((4,)),
+            pltpu.SemaphoreType.DMA((8,)),
             pltpu.SemaphoreType.DMA((2,)),
             pltpu.SemaphoreType.DMA((STEPS,)),
-            pltpu.SemaphoreType.DMA((STEPS, BLOCKS)),
+            pltpu.SemaphoreType.DMA((arrival_slots()[1],)),
             pltpu.SemaphoreType.DMA((3,)),
             pltpu.SemaphoreType.DMA((BLOCKS,)),
             pltpu.SemaphoreType.DMA((2,)),

time: 56.5 us -> 56.4 us (level)
  no operation moved by 1% of the time
where the time goes in v7:
time: 56.4 us; the launch traced here: 55.9 us
  Pallas kernels  53.3 us (95%)
  local copies, waits for them, and re-layouts  1.98 us (4%)
  between operations  0.65 us (1%)
    pallas_call x1, Pallas kernels, main_call(): pl.pallas_call(functools.partial(main_body, maps, cycles, orders), out_sh...  53.3 us
    unnamed x4, local copies, waits for them, and re-layouts  1.98 us

profile of v7, /device:TPU:7, one launch (start us, length us, event | category | flops | bytes accessed | tf_op | source)
XLA Modules:
  0.0 55.9 jit_solution(10692197349263249484)
XLA Ops:
  0.6 0.0 copy-start
  0.6 0.7 %copy-done = s32[512]{0:T(512)S(1)} copy-done((s32[512]{0:T(512)S(1)}, s32[512]{0:T(512)}, u32[]{:S(2)}) %copy-start) | copy-done | bytes 2072
  1.3 53.3 %shard_map.59 = (f32[4,4,2,2048]{3,2,1,0:T(2,128)S(1)}, f32[10,16]{1,0:T(8,128)S(1)}) custom-call(bf16[4,512,2048]{2,1,0:T(8,128)(2,1)} %legendre_ref.1, f32[4,4,4096]{2,1,0:T(4,128)} %sky_ref.1, f32[320,1024]{1,0:T(8,128)} %constant.2.clone.tables_ref, s32[4,128]{1,0:T(4,128)S(1)} %bitcast.1, s32[512]{0:T(512)S(1)} %copy-done), custom_call_target="tpu_custom_call" | custom-call | flops 10000000000 | bytes 16777216 | tf_op jit(solution)/shard_map/pallas_call | solution.py:511
  54.6 0.7 %copy.8 = f32[4,4,2,2048]{3,2,1,0:T(2,128)} copy(f32[4,4,2,2048]{3,2,1,0:T(2,128)S(1)} %get-tuple-element.4) | data formatting | bytes 524288
  55.3 0.6 %copy.9 = f32[10,16]{1,0:T(8,128)} copy(f32[10,16]{1,0:T(8,128)S(1)} %get-tuple-element.5) | data formatting | bytes 1280
Async XLA Ops:
  0.6 0.7 %copy-start = (s32[512]{0:T(512)S(1)}, s32[512]{0:T(512)}, u32[]{:S(2)}) copy-start(s32[512]{0:T(512)} %owner_ref.1) | copy-start | bytes 6148

commit v8 on v7

--- a/solution.py
+++ b/solution.py
@@ -250,7 +250,7 @@
     def core_copy(half, t):
         place_in = (half, slice(None), slice(None), slice(None), pl.ds(*TILES[t]))
         i = (1 - half) * tiles + t
-        return remote(out_core.at[place_in], got.at[place_in], core_send, core_recv.at[i % 8], partner)
+        return remote(out_core.at[place_in], got.at[place_in], core_send, core_recv.at[i % 4], partner)
 
     def make_hot(i):
         column = jnp.transpose(lines[i])[:, 0:1].astype(I32)
@@ -287,11 +287,9 @@
         found = found[0:4] * 16.0 + found[4:8]
         found = jnp.where(lax.broadcasted_iota(I32, (4, 256), 0) == (slot >> 7), found, 0.0)
         lines[i] = jnp.broadcast_to(jnp.sum(found, axis=0, keepdims=True), (8, 256))
-    for i in range(3):
+    for i in range(2):
         make_hot(i)
 
-    pl.semaphore_wait(barrier, len(near))
-    permute(0)
     for load in loads:
         load.wait()
     for t in range(1, tiles):
@@ -306,9 +304,10 @@
         pick = jnp.where(out_row == wanted, 1.0, 0.0).astype(BF16)
         value = value + jnp.dot(pick, spectral[:, q * orders : (q + 1) * orders], preferred_element_type=F32)
     four[...] = value.astype(BF16)
+    pl.semaphore_wait(barrier, len(near))
     four_copy = remote(four, four_got, four_sem.at[0], four_sem.at[1], partner)
     four_copy.start()
-    permute(1)
+    permute(0)
 
     def coefficients(i):
         every = jnp.concatenate([four[...], four_got[...]], axis=0)
@@ -353,8 +352,8 @@
 
     def sums(i):
         half, t = 1 - i // tiles, i % tiles
-        if 0 < i < 2 * tiles - 2:
-            permute(i + 2)
+        if i + 1 < 2 * tiles:
+            permute(i + 1)
         if i == 0:
             four_copy.wait_recv()
             coefficients(0)
@@ -368,13 +367,11 @@
                 acc[at] = value
         if i + 1 < 2 * tiles:
             coefficients(i + 1)
-        if i + 3 < 2 * tiles:
-            make_hot(i + 3)
+        if i + 2 < 2 * tiles:
+            make_hot(i + 2)
         if half:
             for h in range(HALVES):
                 step_copy(0, HALVES * t + h).start()
-        if i == 0:
-            permute(2)
 
     def last_copies(b):
         low, high = ORDERS[b][5], ORDERS[b][4]
@@ -541,7 +538,7 @@
             pltpu.SemaphoreType.DMA((tiles,)),
             pltpu.SemaphoreType.DMA((6,)),
             pltpu.SemaphoreType.DMA,
-            pltpu.SemaphoreType.DMA((8,)),
+            pltpu.SemaphoreType.DMA((4,)),
             pltpu.SemaphoreType.DMA((2,)),
             pltpu.SemaphoreType.DMA((STEPS,)),
             pltpu.SemaphoreType.DMA((arrival_slots()[1],)),

time: 56.4 us -> 55.9 us (level)
  Pallas kernels: 53.3 us -> 52.5 us
    pallas_call x1, Pallas kernels: 53.3 us -> 52.5 us  [main_call(): pl.pallas_call(functools.partial(main_body, maps, cycles, orders), out_sh...]
where the time goes in v8:
time: 55.9 us; the launch traced here: 55.1 us
  Pallas kernels  52.5 us (94%)
  local copies, waits for them, and re-layouts  1.98 us (4%)
  between operations  0.65 us (1%)
    pallas_call x1, Pallas kernels, main_call(): pl.pallas_call(functools.partial(main_body, maps, cycles, orders), out_sh...  52.5 us
    unnamed x4, local copies, waits for them, and re-layouts  1.98 us

profile of v8, /device:TPU:7, one launch (start us, length us, event | category | flops | bytes accessed | tf_op | source)
XLA Modules:
  0.0 55.1 jit_solution(4306206580604162939)
XLA Ops:
  0.6 0.0 copy-start
  0.6 0.7 %copy-done = s32[512]{0:T(512)S(1)} copy-done((s32[512]{0:T(512)S(1)}, s32[512]{0:T(512)}, u32[]{:S(2)}) %copy-start) | copy-done | bytes 2072
  1.3 52.5 %shard_map.59 = (f32[4,4,2,2048]{3,2,1,0:T(2,128)S(1)}, f32[10,16]{1,0:T(8,128)S(1)}) custom-call(bf16[4,512,2048]{2,1,0:T(8,128)(2,1)} %legendre_ref.1, f32[4,4,4096]{2,1,0:T(4,128)} %sky_ref.1, f32[320,1024]{1,0:T(8,128)} %constant.2.clone.tables_ref, s32[4,128]{1,0:T(4,128)S(1)} %bitcast.1, s32[512]{0:T(512)S(1)} %copy-done), custom_call_target="tpu_custom_call" | custom-call | flops 10000000000 | bytes 16777216 | tf_op jit(solution)/shard_map/pallas_call | solution.py:508
  53.8 0.7 %copy.8 = f32[4,4,2,2048]{3,2,1,0:T(2,128)} copy(f32[4,4,2,2048]{3,2,1,0:T(2,128)S(1)} %get-tuple-element.4) | data formatting | bytes 524288
  54.5 0.6 %copy.9 = f32[10,16]{1,0:T(8,128)} copy(f32[10,16]{1,0:T(8,128)S(1)} %get-tuple-element.5) | data formatting | bytes 1280
Async XLA Ops:
  0.6 0.7 %copy-start = (s32[512]{0:T(512)S(1)}, s32[512]{0:T(512)}, u32[]{:S(2)}) copy-start(s32[512]{0:T(512)} %owner_ref.1) | copy-start | bytes 6148
